TPU v7x, 16 devices: a whole 2x2x2 slice. The times are simulated.
16 devices in a mesh: rep: 1, r: 2 (over z), s: 8 (over x, y, core).
Axes of the slice: x: 2, y: 2, z: 2, core: 2. Of those that a mesh axis runs over, the one named last changes fastest.
Arguments:
- x: bfloat16 [16, 2048, 1280], P(('rep', 'r', 's'))
- dy: bfloat16 [16, 2048, 1280], P(('rep', 'r', 's'))
- w_gate: bfloat16 [2, 1280, 4864], P(None, 's')
- w_up: bfloat16 [2, 1280, 4864], P(None, 's')
- w_down: bfloat16 [2, 4864, 1280], P(None, 's')
- m_w_gate: float32 [2, 1280, 4864], P(None, 's')
- m_w_up: float32 [2, 1280, 4864], P(None, 's')
- m_w_down: float32 [2, 4864, 1280], P(None, 's')
- v_w_gate: float32 [2, 1280, 4864], P(None, 's')
- v_w_up: float32 [2, 1280, 4864], P(None, 's')
- v_w_down: float32 [2, 4864, 1280], P(None, 's')
Outputs:
- output 1: bfloat16 [2, 1280, 4864], P('rep', 's')
- output 2: bfloat16 [2, 1280, 4864], P('rep', 's')
- output 3: bfloat16 [2, 4864, 1280], P('rep', 's')
- output 4: float32 [2, 1280, 4864], P('rep', 's')
- output 5: float32 [2, 1280, 4864], P('rep', 's')
- output 6: float32 [2, 4864, 1280], P('rep', 's')
- output 7: float32 [2, 1280, 4864], P('rep', 's')
- output 8: float32 [2, 1280, 4864], P('rep', 's')
- output 9: float32 [2, 4864, 1280], P('rep', 's')
All inputs are finite; a program needn't handle non-finite values.
Results may differ from a plain program's by a relative error of at most 0.0249.
Values are sent between devices in bfloat16 or wider.
A program may use at most 2 GiB of HBM per device.

v0:
```python
import jax
import jax.numpy as jnp
from jax import lax
from jax.sharding import PartitionSpec as P

NAMES = ("w_gate", "w_up", "w_down")


def matmul(a, w):
    return jnp.dot(a, w, preferred_element_type=jnp.float32).astype(jnp.bfloat16)


def normed(h):
    wide = h.astype(jnp.float32)
    scale = lax.rsqrt(jnp.mean(wide**2, -1, keepdims=True) + 1e-6)
    return (wide * scale).astype(jnp.bfloat16)


def layer(h, w):
    a = normed(h)
    gate = jnp.dot(a, w["w_gate"], preferred_element_type=jnp.float32)
    up = jnp.dot(a, w["w_up"], preferred_element_type=jnp.float32)
    return h + matmul((jax.nn.silu(gate) * up).astype(jnp.bfloat16), w["w_down"])


def adamw(w, m, v, g):
    m = 0.9 * m + 0.1 * g
    v = 0.95 * v + 0.05 * g * g
    step = m * lax.rsqrt(v + 1e-8) + 0.1 * w
    return (w - 0.02 * step).astype(jnp.bfloat16), m, v


def solution(mesh):
    def fetched(weights, number):
        return {name: lax.all_gather(w[number], "s", axis=0, tiled=True) for name, w in zip(NAMES, weights, strict=True)}

    def summed(term):
        return lax.psum(lax.psum_scatter(term, "s", scatter_dimension=0, tiled=True), "r")

    def step(x, dy, *arrays):
        weights, m, v = (arrays[i : i + 3] for i in (0, 3, 6))
        layers = weights[0].shape[0]
        h, kept = x[0], []
        for number in range(layers):
            kept.append(h)
            h = layer(h, fetched(weights, number))
        by_h, mine = dy[0], [None] * layers
        for number in reversed(range(layers)):
            _, back = jax.vjp(lambda w, h: layer(h, w), fetched(weights, number), kept[number])
            by_w, by_h = back(by_h)
            mine[number] = [summed(by_w[name]) for name in NAMES]
        gradients = [jnp.stack([mine[number][i] for number in range(layers)]).astype(jnp.float32) for i in range(3)]
        new = [adamw(w.astype(jnp.float32), m, v, g) for w, m, v, g in zip(weights, m, v, gradients, strict=True)]
        return tuple(one[which] for which in range(3) for one in new)

    states, cut = P(("rep", "r", "s"), None, None), P(None, "s", None)
    return jax.shard_map(
        step,
        mesh=mesh,
        in_specs=(states, states) + (cut,) * 9,
        out_specs=(P("rep", "s", None),) * 9,
        check_vma=False,
    )
```

profile of v0, /device:TPU:0, one launch (start us, length us, event | category | flops | bytes accessed | tf_op | source)
XLA Modules:
  0.0 1388.8 jit_solution(4836198576091494971)
XLA Ops:
  7.2 3.9 fusion.99
  11.1 0.0 all-gather.15.cloned.1.call-start
  11.2 3.7 fusion.98
  14.9 0.0 all-gather.17.cloned.1.call-start
  15.0 1.9 fusion.97
  16.9 0.5 all-gather.21.cloned.1.call-update
  17.5 0.5 all-gather.23.cloned.1.call-update
  18.1 0.5 all-gather.19.cloned.1.call-update
  18.7 7.9 copy.20
  26.5 3.6 fusion.36
  30.1 7.9 copy.21
  38.0 43.6 %all-gather.13.cloned.1.call-done = bf16[1,1280,4864]{2,1,0:T(8,128)(2,1)} async-done(((bf16[1,160,4864]{2,1,0:T(8,128)(2,1)}), bf16[1,1280,4864]{2,1,0:T(8,128)(2,1)}) %all-gather.13.cloned.1.call-update) | async-done | bytes 12451856 | tf_op jit(solution)/shard_map/all_gather | solution.py:35
  81.7 34.4 %fusion.34 = f32[2048,4864]{1,0:T(8,128)} fusion(bf16[1,1280,4864]{2,1,0:T(8,128)(2,1)} %all-gather.13.cloned.1.call-done, bf16[1,2048,1280]{1,2,0:T(8,128)(2,1)} %copy.20, f32[2048]{0:T(1024)S(1)} %add_rsqrt_fusion), kind=kOutput, calls=%fused_computation.52 | convolution fusion | flops 25509232640 | bytes 57548800 | tf_op jit(solution)/shard_map/dot_general | solution.py:21
  116.1 35.6 %all-gather.15.cloned.1.call-done = bf16[1,1280,4864]{2,1,0:T(8,128)(2,1)} async-done(((bf16[1,160,4864]{2,1,0:T(8,128)(2,1)}), bf16[1,1280,4864]{2,1,0:T(8,128)(2,1)}) %all-gather.15.cloned.1.call-update) | async-done | bytes 12451856 | tf_op jit(solution)/shard_map/all_gather | solution.py:35
  151.7 48.3 %multiply_convert_fusion.1 = (bf16[2048,4864]{1,0:T(8,128)(2,1)}, f32[2048,4864]{1,0:T(8,128)}) fusion(f32[2048,4864]{1,0:T(8,128)} %fusion.34, bf16[1,1280,4864]{2,1,0:T(8,128)(2,1)} %all-gather.15.cloned.1.call-done, bf16[1,2048,1280]{1,2,0:T(8,128)(2,1)} %copy.20, f32[2048]{0:T(1024)S(1)} %add_rsqrt_fusion), kind=kOutput, calls=%fused_computation.17 | convolution fusion | flops 25569001472 | bytes 117317632 | tf_op jit(solution)/shard_map/dot_general | solution.py:22
  200.0 21.7 %all-gather.17.cloned.1.call-done = bf16[1,4864,1280]{2,1,0:T(8,128)(2,1)} async-done(((bf16[1,608,1280]{2,1,0:T(8,128)(2,1)}), bf16[1,4864,1280]{2,1,0:T(8,128)(2,1)}) %all-gather.17.cloned.1.call-update) | async-done | bytes 12451856 | tf_op jit(solution)/shard_map/all_gather | solution.py:35
  221.7 46.0 %fusion.40 = (f32[2048]{0:T(1024)S(1)}, bf16[2048,1280]{0,1:T(8,128)(2,1)}) fusion(bf16[2048,4864]{1,0:T(8,128)(2,1)} %get-tuple-element.30, bf16[1,4864,1280]{2,1,0:T(8,128)(2,1)} %all-gather.17.cloned.1.call-done, bf16[1,2048,1280]{1,2,0:T(8,128)(2,1)} %copy.20), kind=kOutput, calls=%fused_computation.58 | convolution fusion | flops 25514473472 | bytes 42868736 | tf_op jit(solution)/shard_map/dot_general | solution.py:10
  267.7 0.6 copy-done.11
  268.3 23.2 %all-gather.21.cloned.1.call-done = bf16[1,4864,1280]{2,1,0:T(8,128)(2,1)} async-done(((bf16[1,608,1280]{2,1,0:T(8,128)(2,1)}), bf16[1,4864,1280]{2,1,0:T(8,128)(2,1)}) %all-gather.21.cloned.1.call-update) | async-done | bytes 12451856 | tf_op jit(solution)/shard_map/all_gather | solution.py:35
  291.5 34.2 %convolution_convert_fusion.1 = bf16[2048,4864]{1,0:T(8,128)(2,1)} fusion(bf16[1,4864,1280]{2,1,0:T(8,128)(2,1)} %all-gather.21.cloned.1.call-done, bf16[1,2048,1280]{2,1,0:T(8,128)(2,1)} %param.12), kind=kOutput, calls=%fused_computation.29 | convolution fusion | flops 25511329792 | bytes 37617664 | tf_op jit(solution)/shard_map/transpose(jvp())/dot_general | solution.py:10
  325.7 35.6 %all-gather.23.cloned.1.call-done = bf16[1,1280,4864]{2,1,0:T(8,128)(2,1)} async-done(((bf16[1,160,4864]{2,1,0:T(8,128)(2,1)}), bf16[1,1280,4864]{2,1,0:T(8,128)(2,1)}) %all-gather.23.cloned.1.call-update) | async-done | bytes 12451856 | tf_op jit(solution)/shard_map/all_gather | solution.py:35
  361.4 34.4 %fusion.21 = f32[2048,4864]{1,0:T(8,128)} fusion(bf16[1,1280,4864]{2,1,0:T(8,128)(2,1)} %all-gather.23.cloned.1.call-done, bf16[2048,1280]{0,1:T(8,128)(2,1)} %get-tuple-element.33, f32[2048]{0:T(1024)S(1)} %fusion.85), kind=kOutput, calls=%fused_computation.39 | convolution fusion | flops 25509232640 | bytes 57548800 | tf_op jit(solution)/shard_map/jvp()/dot_general | solution.py:22
  395.8 35.4 %all-gather.19.cloned.1.call-done = bf16[1,1280,4864]{2,1,0:T(8,128)(2,1)} async-done(((bf16[1,160,4864]{2,1,0:T(8,128)(2,1)}), bf16[1,1280,4864]{2,1,0:T(8,128)(2,1)}) %all-gather.19.cloned.1.call-update) | async-done | bytes 12451856 | tf_op jit(solution)/shard_map/all_gather | solution.py:35
  431.2 55.4 %fusion.2 = (bf16[2048,4864]{1,0:T(8,128)(2,1)}, f32[2048,4864]{1,0:T(8,128)}) fusion(f32[2048,4864]{1,0:T(8,128)} %fusion.21, bf16[2048,4864]{1,0:T(8,128)(2,1)} %convolution_convert_fusion.1, bf16[1,1280,4864]{2,1,0:T(8,128)(2,1)} %all-gather.19.cloned.1.call-done, bf16[2048,1280]{0,1:T(8,128)(2,1)} %get-tuple-element.33, f32[2048]{0:T(1024)S(1)} %fusion.85), kind=kOutput, calls=%fused_computation.8 | convolution fusion | flops 25628770304 | bytes 137240576 | tf_op jit(solution)/shard_map/jvp()/dot_general | solution.py:21
  486.6 37.0 %fusion.46 = bf16[2048,1280]{0,1:T(8,128)(2,1)} fusion(bf16[1,1280,4864]{2,1,0:T(8,128)(2,1)} %all-gather.23.cloned.1.call-done, bf16[2048,4864]{1,0:T(8,128)(2,1)} %convolution_convert_fusion.1, f32[2048,4864]{1,0:T(8,128)} %get-tuple-element.35), kind=kOutput, calls=%fused_computation.74 | convolution fusion | flops 25563758592 | bytes 77463552 | tf_op jit(solution)/shard_map/transpose(jvp())/dot_general | solution.py:22
  523.6 36.0 %fusion.42 = (f32[2048]{0:T(1024)S(1)}, bf16[2048,1280]{0,1:T(8,128)(2,1)}) fusion(bf16[2048,1280]{0,1:T(8,128)(2,1)} %get-tuple-element.33, bf16[2048,1280]{0,1:T(8,128)(2,1)} %fusion.46, bf16[2048,4864]{1,0:T(8,128)(2,1)} %get-tuple-element.34, bf16[1,1280,4864]{2,1,0:T(8,128)(2,1)} %all-gather.19.cloned.1.call-done), kind=kOutput, calls=%fused_computation.60 | convolution fusion | flops 25514473472 | bytes 48111616 | tf_op jit(solution)/shard_map/transpose(jvp())/dot_general | solution.py:21
  559.6 12.4 fusion.74
  572.0 33.9 %convolution_convert_fusion.2 = bf16[4864,1280]{1,0:T(8,128)(2,1)} fusion(bf16[2048,4864]{1,0:T(8,128)(2,1)} %get-tuple-element.30, bf16[2048,1280]{0,1:T(8,128)(2,1)} %fusion.74), kind=kOutput, calls=%fused_computation.30 | convolution fusion | flops 25507594240 | bytes 37617664 | tf_op jit(solution)/shard_map/transpose(jvp())/dot_general | solution.py:10
  605.8 0.0 reduce-scatter.17.cloned.1.call-start
  605.9 41.6 %fusion.18 = bf16[4864,1280]{1,0:T(8,128)(2,1)} fusion(f32[2048,4864]{1,0:T(8,128)} %fusion.21, bf16[1,2048,1280]{2,1,0:T(8,128)(2,1)} %param.12, f32[2048,4864]{1,0:T(8,128)} %get-tuple-element.35), kind=kOutput, calls=%fused_computation.25 | convolution fusion | flops 25567363072 | bytes 97386496 | tf_op jit(solution)/shard_map/transpose(jvp())/dot_general | solution.py:10
  647.5 0.0 reduce-scatter.11.cloned.1.call-start
  647.6 34.1 %convolution_convert_fusion = bf16[2048,4864]{1,0:T(8,128)(2,1)} fusion(bf16[2048,1280]{0,1:T(8,128)(2,1)} %fusion.74, bf16[1,4864,1280]{2,1,0:T(8,128)(2,1)} %all-gather.17.cloned.1.call-done), kind=kOutput, calls=%fused_computation.28 | convolution fusion | flops 25511329792 | bytes 37617664 | tf_op jit(solution)/shard_map/transpose(jvp())/dot_general | solution.py:10
  681.6 37.8 %fusion.20 = bf16[1280,4864]{1,0:T(8,128)(2,1)} fusion(bf16[2048,4864]{1,0:T(8,128)(2,1)} %convolution_convert_fusion, f32[2048,4864]{1,0:T(8,128)} %fusion.34, bf16[1,2048,1280]{1,2,0:T(8,128)(2,1)} %copy.20, f32[2048]{0:T(1024)S(1)} %copy-done.14), kind=kOutput, calls=%fused_computation.27 | convolution fusion | flops 25575227392 | bytes 77471744 | tf_op jit(solution)/shard_map/transpose(jvp())/dot_general | solution.py:22
  719.5 0.0 reduce-scatter.13.cloned.1.call-start
  719.5 0.6 copy-done.10
  720.1 37.9 %fusion.19 = bf16[1280,4864]{1,0:T(8,128)(2,1)} fusion(bf16[2048,4864]{1,0:T(8,128)(2,1)} %convolution_convert_fusion.1, bf16[2048,1280]{0,1:T(8,128)(2,1)} %get-tuple-element.33, f32[2048]{0:T(1024)S(1)} %copy-done.10, f32[2048,4864]{1,0:T(8,128)} %get-tuple-element.35), kind=kOutput, calls=%fused_computation.26 | convolution fusion | flops 25575227392 | bytes 77471744 | tf_op jit(solution)/shard_map/transpose(jvp())/dot_general | solution.py:22
  758.1 0.0 reduce-scatter.7.cloned.1.call-start
  758.1 48.0 %fusion.15 = bf16[1280,4864]{1,0:T(8,128)(2,1)} fusion(f32[2048,4864]{1,0:T(8,128)} %fusion.34, f32[2048,4864]{1,0:T(8,128)} %get-tuple-element.31, bf16[2048,4864]{1,0:T(8,128)(2,1)} %convolution_convert_fusion, bf16[1,2048,1280]{1,2,0:T(8,128)(2,1)} %copy.20, f32[2048]{0:T(1024)S(1)} %copy-done.14), kind=kOutput, calls=%fused_computation.24 | convolution fusion | flops 25625034752 | bytes 117317632 | tf_op jit(solution)/shard_map/transpose(jvp())/dot_general | solution.py:21
  806.2 33.2 %convolution_convert_fusion.3 = bf16[1280,4864]{1,0:T(8,128)(2,1)} fusion(bf16[2048,4864]{1,0:T(8,128)(2,1)} %get-tuple-element.34, bf16[2048,1280]{0,1:T(8,128)(2,1)} %get-tuple-element.33, f32[2048]{0:T(1024)S(1)} %copy-done.10), kind=kOutput, calls=%fused_computation.31 | convolution fusion | flops 25509232640 | bytes 37625856 | tf_op jit(solution)/shard_map/transpose(jvp())/dot_general | solution.py:21
  839.5 27.0 %reduce-scatter.11.cloned.1.call-done = bf16[160,4864]{1,0:T(8,128)(2,1)} async-done(((bf16[1280,4864]{1,0:T(8,128)(2,1)}), bf16[160,4864]{1,0:T(8,128)(2,1)}) %reduce-scatter.11.cloned.1.call-update) | async-done | bytes 1556496 | tf_op jit(solution)/shard_map/reduce_scatter | solution.py:38
  866.5 87.9 %reduce-scatter.13.cloned.1.call-done = bf16[160,4864]{1,0:T(8,128)(2,1)} async-done(((bf16[1280,4864]{1,0:T(8,128)(2,1)}), bf16[160,4864]{1,0:T(8,128)(2,1)}) %reduce-scatter.13.cloned.1.call-update) | async-done | bytes 1556496 | tf_op jit(solution)/shard_map/reduce_scatter | solution.py:38
  954.4 88.1 %reduce-scatter.7.cloned.1.call-done = bf16[160,4864]{1,0:T(8,128)(2,1)} async-done(((bf16[1280,4864]{1,0:T(8,128)(2,1)}), bf16[160,4864]{1,0:T(8,128)(2,1)}) %reduce-scatter.7.cloned.1.call-update) | async-done | bytes 1556496 | tf_op jit(solution)/shard_map/reduce_scatter | solution.py:38
  1042.5 87.9 %reduce-scatter.9.cloned.1.call-done = bf16[160,4864]{1,0:T(8,128)(2,1)} async-done(((bf16[1280,4864]{1,0:T(8,128)(2,1)}), bf16[160,4864]{1,0:T(8,128)(2,1)}) %reduce-scatter.9.cloned.1.call-update) | async-done | bytes 1556496 | tf_op jit(solution)/shard_map/reduce_scatter | solution.py:38
  1130.4 217.7 %all-reduce.3.cloned.1.call-done = (bf16[1,160,4864]{2,1,0:T(8,128)(2,1)}, bf16[1,160,4864]{2,1,0:T(8,128)(2,1)}, bf16[1,160,4864]{2,1,0:T(8,128)(2,1)}, bf16[1,...) async-done(((bf16[1,160,4864]{2,1,0:T(8,128)(2,1)}, bf16[1,160,4864]{2,1,0:T(8,128)(2,1)}, bf16[1,160,4864]{2,1,0:T(8,128)(2,1)}, ...) | async-done | bytes 9338896 | tf_op jit(solution)/shard_map/psum | solution.py:38
  1348.1 13.1 fusion.69
  1361.3 0.5 copy-done.6
  1361.7 0.8 copy-done.7
  1362.5 19.2 %fusion.61 = (bf16[2,160,4864]{2,1,0:T(8,128)(2,1)}, f32[2,160,4864]{2,1,0:T(8,128)}, f32[2,160,4864]{2,1,0:T(8,128)}, bf16[2,160,4864]{2,1,0:T(8,128)(2,1)}, f3...) fusion(bf16[2,160,4864]{2,1,0:T(8,128)(2,1)S(1)} %copy-done.2, bf16[1,160,4864]{2,1,0:T(8,128)(2,1)S(1)} %copy-done.4, ...), kind=kLoop, calls=%fused_computation.80 | loop fusion | flops 59146240 | bytes 68485120 | tf_op jit(solution)/shard_map/convert_element_type | solution.py:30
  (48 shorter events, 0.6 us)
Async XLA Ops:
  7.2 7.8 copy-start
  7.2 74.5 %all-gather.13.cloned.1.call-start = ((), (), s32[]{:S(2)}) async-start(), calls=%async_computation.12 | async-start | bytes 14008320 | tf_op jit(solution)/shard_map/all_gather | solution.py:35
  11.1 140.5 %all-gather.15.cloned.1.call-start = ((), (), s32[]{:S(2)}) async-start(), calls=%async_computation.13 | async-start | bytes 14008320 | tf_op jit(solution)/shard_map/all_gather | solution.py:35
  14.9 206.7 %all-gather.17.cloned.1.call-start = ((), (), s32[]{:S(2)}) async-start(), calls=%async_computation.14 | async-start | bytes 14008320 | tf_op jit(solution)/shard_map/all_gather | solution.py:35
  16.9 274.7 %all-gather.21.cloned.1.call-start = ((), (), s32[]{:S(2)}) async-start(), calls=%async_computation.16 | async-start | bytes 14008320 | tf_op jit(solution)/shard_map/all_gather | solution.py:35
  17.4 343.9 %all-gather.23.cloned.1.call-start = ((), (), s32[]{:S(2)}) async-start(), calls=%async_computation.17 | async-start | bytes 14008320 | tf_op jit(solution)/shard_map/all_gather | solution.py:35
  18.0 413.2 %all-gather.19.cloned.1.call-start = ((), (), s32[]{:S(2)}) async-start(), calls=%async_computation.15 | async-start | bytes 14008320 | tf_op jit(solution)/shard_map/all_gather | solution.py:35
  18.6 820.9 %reduce-scatter.15.cloned.1.call-start = ((), (), s32[]{:S(2)}) async-start(), calls=%async_computation.10 | async-start | bytes 14008320 | tf_op jit(solution)/shard_map/reduce_scatter | solution.py:38
  30.1 121.5 %copy-start.13 = (f32[2048]{0:T(1024)}, f32[2048]{0:T(1024)S(1)}, u32[]{:S(2)}) copy-start(f32[2048]{0:T(1024)S(1)} %add_rsqrt_fusion) | copy-start | bytes 24580
  267.7 0.6 copy-start.11
  268.3 162.9 %copy-start.8 = (f32[2048]{0:T(1024)}, f32[2048]{0:T(1024)S(1)}, u32[]{:S(2)}) copy-start(f32[2048]{0:T(1024)S(1)} %fusion.85) | copy-start | bytes 24580
  523.6 36.0 %copy-start.12 = (f32[2048]{0:T(1024)S(1)}, f32[2048]{0:T(1024)}, u32[]{:S(2)}) copy-start(f32[2048]{0:T(1024)} %copy-done.11) | copy-start | bytes 24580
  523.6 36.0 %copy-start.9 = (f32[2048]{0:T(1024)S(1)}, f32[2048]{0:T(1024)}, u32[]{:S(2)}) copy-start(f32[2048]{0:T(1024)} %copy-done.8) | copy-start | bytes 24580
  605.8 233.7 %reduce-scatter.17.cloned.1.call-start = ((), (), s32[]{:S(2)}) async-start(), calls=%async_computation.11 | async-start | bytes 14008320 | tf_op jit(solution)/shard_map/reduce_scatter | solution.py:38
  647.5 34.1 %copy-start.14 = (f32[2048]{0:T(1024)S(1)}, f32[2048]{0:T(1024)}, u32[]{:S(2)}) copy-start(f32[2048]{0:T(1024)} %copy-done.13) | copy-start | bytes 24580
  647.5 219.0 %reduce-scatter.11.cloned.1.call-start = ((), (), s32[]{:S(2)}) async-start(), calls=%async_computation.8 | async-start | bytes 14008320 | tf_op jit(solution)/shard_map/reduce_scatter | solution.py:38
  719.4 0.7 copy-start.10
  719.5 235.0 %reduce-scatter.13.cloned.1.call-start = ((), (), s32[]{:S(2)}) async-start(), calls=%async_computation.9 | async-start | bytes 14008320 | tf_op jit(solution)/shard_map/reduce_scatter | solution.py:38
  758.1 284.4 %reduce-scatter.7.cloned.1.call-start = ((), (), s32[]{:S(2)}) async-start(), calls=%async_computation.6 | async-start | bytes 14008320 | tf_op jit(solution)/shard_map/reduce_scatter | solution.py:38
  806.1 324.3 %reduce-scatter.9.cloned.1.call-start = ((), (), s32[]{:S(2)}) async-start(), calls=%async_computation.7 | async-start | bytes 14008320 | tf_op jit(solution)/shard_map/reduce_scatter | solution.py:38
  839.4 508.7 %copy-start.1 = (bf16[2,608,1280]{2,1,0:T(8,128)(2,1)S(1)}, bf16[2,608,1280]{2,1,0:T(8,128)(2,1)}, u32[]{:S(2)}) copy-start(bf16[2,608,1280]{2,1,0:T(8,128)(2,1)} %param.15) | copy-start | bytes 9338884
  839.4 508.6 %all-reduce.3.cloned.1.call-start = ((), (), s32[]{:S(2)}) async-start(), calls=%async_computation.18 | async-start | bytes 18677760 | tf_op jit(solution)/shard_map/psum | solution.py:38
  1348.1 13.2 copy-start.2
  1348.1 13.2 copy-start.3
  1348.1 13.2 copy-start.4
  1348.1 13.2 copy-start.5
  1348.1 13.7 copy-start.6
  1348.1 14.4 %copy-start.7 = (bf16[1,160,4864]{2,1,0:T(8,128)(2,1)S(1)}, bf16[1,160,4864]{2,1,0:T(8,128)(2,1)}, u32[]{:S(2)}) copy-start(bf16[1,160,4864]{2,1,0:T(8,128)(2,1)} %get-tuple-element.12) | copy-start | bytes 4669444
Sparse Core Ops, SparseCore 0:
  11.2 70.3 all-gather.12
  84.1 67.5 all-gather.14
  154.1 67.5 all-gather.16
  223.9 67.5 all-gather.20
  293.8 67.5 all-gather.22
  363.6 67.5 all-gather.18
  606.0 84.3 reduce-scatter.14
  694.0 84.4 reduce-scatter.16
  782.1 84.3 reduce-scatter.10
  870.0 84.3 reduce-scatter.12
  958.0 84.3 reduce-scatter.6
  1045.9 84.3 reduce-scatter.8
  1133.5 214.5 all-reduce.2
where the time goes:
time: 1400 us; the launch traced here: 1390 us
  waiting for transfers between devices  705 us (50%)
  matrix products  592 us (42%)
  other arithmetic  48.3 us (3%)
  local copies, waits for them, and re-layouts  27.7 us (2%)
  between operations  14.6 us (1%)
    reduce_scatter x6, waiting for transfers between devices, summed(): lax.psum_scatter(term, 's', scatter_dimension=0, tiled=True)  291 us
    psum x1, waiting for transfers between devices, summed(): lax.psum(lax.psum_scatter(term, 's', scatter_dimension=0, tiled=True), 'r')  218 us
    dot_general x5, matrix products, layer(): gate = jnp.dot(a, w['w_gate'], preferred_element_type=jnp.float32)  207 us
    dot_general x5, matrix products, layer(): up = jnp.dot(a, w['w_up'], preferred_element_type=jnp.float32)  195 us
    all_gather x6, waiting for transfers between devices, fetched(): lax.all_gather(w[number], 's', axis=0, tiled=True)  195 us
    dot_general x5, matrix products, matmul(): jnp.dot(a, w, preferred_element_type=jnp.float32).astype(jnp.bfloat16)  190 us
    convert_element_type x2, other arithmetic, adamw(): return ((w - 0.02 * step).astype(jnp.bfloat16), m, v)  32.3 us
  transfers between devices with their start and end apart: 13, of which 11 were waited for; matrix products, arithmetic and copies ran while one was open for 33% of the time, Pallas kernels for 0%

commit v1 on v0

v1 whole, which is shorter than its diff:
```python
import functools

import jax
import jax.numpy as jnp
from jax import lax
from jax.experimental import pallas as pl
from jax.experimental.pallas import tpu as pltpu
from jax.sharding import PartitionSpec as P

BF16, F32 = jnp.bfloat16, jnp.float32
LIMIT = 61 * 1024 * 1024
ANY = pl.BlockSpec(memory_space=pl.ANY)


def normed(h):
    wide = h.astype(jnp.float32)
    scale = lax.rsqrt(jnp.mean(wide**2, -1, keepdims=True) + 1e-6)
    return (wide * scale).astype(jnp.bfloat16)


def adamw(w, m, v, g):
    m = 0.9 * m + 0.1 * g
    v = 0.95 * v + 0.05 * g * g
    step = m * lax.rsqrt(v + 1e-8) + 0.1 * w
    return (w - 0.02 * step).astype(jnp.bfloat16), m, v


def wide(value):
    return value.astype(F32)


def narrow(value):
    return value.astype(BF16)


def place():
    me = lax.axis_index("s")
    return me // 4, (me // 2) % 2, me % 2


def index_of(*changed):
    x, y, c = place()
    x, y, c = (1 - v if k in changed else v for k, v in (("x", x), ("y", y), ("c", c)))
    return x * 4 + y * 2 + c


def square_of(*changed):
    x, y, _ = place()
    x, y = (1 - v if k in changed else v for k, v in (("x", x), ("y", y)))
    return x * 2 + y


def device(way):
    return {"r": 1 - lax.axis_index("r")} if way == "z" else {"s": index_of(way)}


class Sends:
    def __init__(self, send_sem, recv_sem):
        self.send_sem, self.recv_sem, self.made = send_sem, recv_sem, {}

    def copy(self, number, way, src, dst):
        return pltpu.make_async_remote_copy(
            src_ref=src, dst_ref=dst, send_sem=self.send_sem.at[number], recv_sem=self.recv_sem.at[number],
            device_id=device(way), device_id_type=pl.DeviceIdType.MESH,
        )


class Gather:
    ways, copies, stages = ("x", "y", "c"), 8, 2

    def __init__(self, block):
        self.operands = (block,)
        self.shapes = (jax.ShapeDtypeStruct((8,) + block.shape, block.dtype),)
        self.half = block.shape[0] // 2

    def parts(self, sends, ins, outs):
        (b,), (g,) = ins, outs
        h = self.half
        me, by_x, by_y, by_xy = index_of(), index_of("x"), index_of("y"), index_of("x", "y")
        low, high = pl.ds(0, h), pl.ds(h, h)
        return [
            sends.copy(0, "x", b, g.at[me]),
            sends.copy(1, "y", b, g.at[me]),
            sends.copy(2, "c", b, g.at[me]),
            sends.copy(3, "y", g.at[by_x, low], g.at[by_x, low]),
            sends.copy(4, "x", g.at[by_y, high], g.at[by_y, high]),
            sends.copy(5, "c", g.at[by_x], g.at[by_x]),
            sends.copy(6, "c", g.at[by_y], g.at[by_y]),
            sends.copy(7, "c", g.at[by_xy], g.at[by_xy]),
        ]

    def stage(self, number, sends, ins, outs, local):
        part = self.parts(sends, ins, outs)
        own = pltpu.make_async_copy(ins[0], outs[0].at[index_of()], local)
        if number == 0:
            own.start()
            for each in part[:3]:
                each.start()
        elif number == 1:
            part[0].wait_recv()
            part[1].wait_recv()
            for each in part[3:7]:
                each.start()
        else:
            part[3].wait_recv()
            part[4].wait_recv()
            part[7].start()
            own.wait()
            for each in (2, 5, 6, 7):
                part[each].wait_recv()
            for each in part:
                each.wait_send()


class Scatter1:
    ways, copies, stages = ("x", "y"), 4, 1

    def __init__(self, sums):
        self.operands = (sums,)
        self.half = sums.shape[1] // 2
        shape = jax.ShapeDtypeStruct((2, self.half) + sums.shape[2:], sums.dtype)
        self.shapes = (shape, shape)

    def parts(self, sends, ins, outs):
        (s,), (rx, ry) = ins, outs
        low, high = pl.ds(0, self.half), pl.ds(self.half, self.half)
        far = square_of("x", "y")
        return [
            sends.copy(0, "x", s.at[far, low], rx.at[1]),
            sends.copy(1, "y", s.at[far, high], ry.at[1]),
            sends.copy(2, "x", s.at[square_of("x"), low], rx.at[0]),
            sends.copy(3, "y", s.at[square_of("y"), high], ry.at[0]),
        ]

    def stage(self, number, sends, ins, outs, local):
        for each in self.parts(sends, ins, outs):
            each.start() if number == 0 else each.wait()


class Scatter2(Scatter1):
    ways, copies, stages = ("x", "y"), 2, 1

    def __init__(self, to_y, to_x):
        self.operands = (to_y, to_x)
        self.shapes = tuple(jax.ShapeDtypeStruct(t.shape, t.dtype) for t in (to_y, to_x))

    def parts(self, sends, ins, outs):
        return [sends.copy(0, "y", ins[0], outs[0]), sends.copy(1, "x", ins[1], outs[1])]


class Across(Scatter1):
    ways, copies, stages = ("z",), 1, 1

    def __init__(self, block):
        self.operands = (block,)
        self.shapes = (jax.ShapeDtypeStruct(block.shape, block.dtype),)

    def parts(self, sends, ins, outs):
        return [sends.copy(0, "z", ins[0], outs[0])]


class Line:
    def __init__(self):
        self.calls, self.last = 0, None

    def call(self, name, body, steps, operands, in_specs, shapes, out_specs, scratch=(), ways=(), tasks=(), flops=0):
        tasks = list(tasks)
        ways = tuple(sorted(set(ways).union(*(t.ways for t in tasks))))
        counts = [len(operands), sum(len(t.operands) for t in tasks), len(shapes), sum(len(t.shapes) for t in tasks), len(scratch)]

        def kernel(*refs):
            refs = list(refs)
            ins, task_ins, outs, task_outs, own = ([refs.pop(0) for _ in range(n)] for n in counts)
            i = pl.program_id(0)
            held = []
            for t in tasks:
                a, task_ins = task_ins[: len(t.operands)], task_ins[len(t.operands) :]
                b, task_outs = task_outs[: len(t.shapes)], task_outs[len(t.shapes) :]
                sems, refs = refs[:3], refs[3:]
                held.append((t, Sends(sems[0], sems[1]), a, b, sems[2]))

            if ways:
                @pl.when(i == 0)
                def _():
                    barrier = pltpu.get_barrier_semaphore()
                    for way in ways:
                        pl.semaphore_signal(barrier, inc=1, device_id=device(way), device_id_type=pl.DeviceIdType.MESH)
                    pl.semaphore_wait(barrier, len(ways))
                    for t, sends, a, b, local in held:
                        t.stage(0, sends, a, b, local)

            for t, sends, a, b, local in held:
                for number in range(1, t.stages):
                    @pl.when(i == (steps * number * 2) // (t.stages * 2 - 1))
                    def _():
                        t.stage(number, sends, a, b, local)

            if body is not None:
                body(i, ins, outs, own)

            if held:
                @pl.when(i == steps - 1)
                def _():
                    for t, sends, a, b, local in held:
                        t.stage(t.stages, sends, a, b, local)

        sems = []
        for t in tasks:
            sems += [pltpu.SemaphoreType.DMA((t.copies,)), pltpu.SemaphoreType.DMA((t.copies,)), pltpu.SemaphoreType.DMA]
        task_operands = tuple(o for t in tasks for o in t.operands)
        task_shapes = tuple(s for t in tasks for s in t.shapes)
        given = tuple(operands) + task_operands
        if self.last is not None:
            given, _ = lax.optimization_barrier((given, self.last))
        params = {"collective_id": self.calls, "has_side_effects": True} if ways else {}
        results = pl.pallas_call(
            kernel,
            grid=(steps,),
            out_shape=tuple(shapes) + task_shapes,
            in_specs=list(in_specs) + [ANY] * len(task_operands),
            out_specs=list(out_specs) + [ANY] * len(task_shapes),
            scratch_shapes=list(scratch) + sems,
            name=name,
            compiler_params=pltpu.CompilerParams(dimension_semantics=("arbitrary",), vmem_limit_bytes=LIMIT, **params),
            cost_estimate=pl.CostEstimate(flops=flops, bytes_accessed=0, transcendentals=0),
        )(*given)
        self.calls += 1
        self.last = results[0]
        own, rest = results[: len(shapes)], list(results[len(shapes) :])
        moved = [[rest.pop(0) for _ in t.shapes] for t in tasks]
        return own, moved


def shape(*dims, dtype=BF16):
    return jax.ShapeDtypeStruct(dims, dtype)


def held_block(dims):
    return pl.BlockSpec(dims, lambda i: (0,) * len(dims), pipeline_mode=pl.Buffered(1))


def dot(a, b, contract=(1, 0)):
    return lax.dot_general(a, b, (((contract[0],), (contract[1],)), ((), ())), preferred_element_type=F32)


WIDTH = 256
TALL = 256


def norm_call(line, h, tasks):
    t, d = h.shape

    def body(i, ins, outs, own):
        a = normed(ins[0][...])
        outs[0][...] = a
        outs[1][...] = a.T

    return line.call(
        "norm", body, t // TALL, (h,), [pl.BlockSpec((TALL, d), lambda i: (i, 0))], (shape(t, d), shape(d, t)),
        [pl.BlockSpec((TALL, d), lambda i: (i, 0)), pl.BlockSpec((d, TALL), lambda i: (0, i))], tasks=tasks,
    )


def gate_call(line, a, w, tasks):
    t, d = a.shape
    f = w.shape[1]

    def body(i, ins, outs, own):
        outs[0][...] = dot(ins[0][...], ins[1][...])

    return line.call(
        "gate", body, f // WIDTH, (a, w), [held_block((t, d)), pl.BlockSpec((d, WIDTH), lambda i: (0, i))],
        (shape(t, f, dtype=F32),), [pl.BlockSpec((t, WIDTH), lambda i: (0, i))], tasks=tasks, flops=2 * t * d * f,
    )


def up_call(line, a, w, gate, tasks):
    t, d = a.shape
    f = w.shape[1]
    tile = pl.BlockSpec((t, WIDTH), lambda i: (0, i))

    def body(i, ins, outs, own):
        up = dot(ins[0][...], ins[1][...])
        outs[0][...] = up
        act = narrow(jax.nn.silu(ins[2][...]) * up)
        outs[1][...] = act
        outs[2][...] = act.T

    return line.call(
        "up", body, f // WIDTH, (a, w, gate), [held_block((t, d)), pl.BlockSpec((d, WIDTH), lambda i: (0, i)), tile],
        (shape(t, f, dtype=F32), shape(t, f), shape(f, t)), [tile, tile, pl.BlockSpec((WIDTH, t), lambda i: (i, 0))],
        tasks=tasks, flops=2 * t * d * f,
    )


def down_call(line, act, w, h, tasks):
    t, f = act.shape
    d = w.shape[1]
    rows = lambda n: pl.BlockSpec((TALL, n), lambda i: (i, 0))

    def body(i, ins, outs, own):
        new = ins[2][...] + narrow(dot(ins[0][...], ins[1][...]))
        outs[0][...] = new
        a = normed(new)
        outs[1][...] = a
        outs[2][...] = a.T

    return line.call(
        "down", body, t // TALL, (act, w, h), [rows(f), held_block((f, d)), rows(d)], (shape(t, d), shape(t, d), shape(d, t)),
        [rows(d), rows(d), pl.BlockSpec((d, TALL), lambda i: (0, i))], tasks=tasks, flops=2 * t * d * f,
    )


def by_act_call(line, by_h, w, gate, up, tasks):
    t, d = by_h.shape
    f = w.shape[0]
    tile = pl.BlockSpec((t, WIDTH), lambda i: (0, i))

    def body(i, ins, outs, own):
        by_act = wide(narrow(dot(ins[0][...], ins[1][...], (1, 1))))
        gate = ins[2][...]
        share = jax.nn.sigmoid(gate)
        silu = gate * share
        outs[0][...] = narrow(by_act * ins[3][...] * (share + silu * (1 - share)))
        outs[1][...] = narrow(by_act * silu)

    return line.call(
        "by_act", body, f // WIDTH, (by_h, w, gate, up), [held_block((t, d)), pl.BlockSpec((WIDTH, d), lambda i: (i, 0)), tile, tile],
        (shape(t, f), shape(t, f)), [tile, tile], tasks=tasks, flops=2 * t * d * f,
    )


def by_a_call(line, by, w, before, tasks):
    t, f = by.shape
    d = w.shape[0]
    rows = lambda n: pl.BlockSpec((TALL, n), lambda i: (i, 0))
    more = () if before is None else (before,)

    def body(i, ins, outs, own):
        new = narrow(dot(ins[0][...], ins[1][...], (1, 1)))
        if more:
            new = narrow(wide(new) + wide(ins[2][...]))
        outs[0][...] = new

    return line.call(
        "by_a", body, t // TALL, (by, w) + more, [rows(f), held_block((d, f))] + [rows(d)] * len(more), (shape(t, d),), [rows(d)],
        tasks=tasks, flops=2 * t * d * f,
    )


def by_wide_call(line, a_t, by, tasks):
    d, t = a_t.shape
    f = by.shape[1]
    rows, tiles = d // 8, f // WIDTH

    def body(i, ins, outs, own):
        mine, theirs, send_sem, recv_sem = own
        c = place()[2]

        def sent(n):
            return pltpu.make_async_remote_copy(
                src_ref=mine.at[n % 3, 1 - c], dst_ref=theirs.at[n], send_sem=send_sem.at[n % 3], recv_sem=recv_sem.at[n],
                device_id=device("c"), device_id_type=pl.DeviceIdType.MESH,
            )

        @pl.when((i >= 1) & (i <= tiles))
        def _():
            sent(i - 1).start()

        @pl.when(i < tiles)
        def _():
            new = narrow(dot(ins[0][...], ins[1][...])).reshape(4, 2, rows, WIDTH)
            slot = i % 3
            mine[slot, 0] = new[:, 0]
            mine[slot, 1] = new[:, 1]

        @pl.when(i >= 2)
        def _():
            n = i - 2
            sent(n).wait()
            outs[0][...] = narrow(wide(mine[n % 3, c]) + wide(theirs[n]))

    return line.call(
        "by_wide", body, tiles + 2, (a_t, by), [held_block((d, t)), pl.BlockSpec((t, WIDTH), lambda i: (0, jnp.minimum(i, tiles - 1)))],
        (shape(4, rows, f),), [pl.BlockSpec((4, rows, WIDTH), lambda i: (0, 0, jnp.maximum(i - 2, 0)))],
        scratch=[
            pltpu.VMEM((3, 2, 4, rows, WIDTH), BF16), pltpu.VMEM((tiles, 4, rows, WIDTH), BF16),
            pltpu.SemaphoreType.DMA((3,)), pltpu.SemaphoreType.DMA((tiles,)),
        ],
        ways=("c",), tasks=tasks, flops=2 * t * d * f,
    )


def by_down_call(line, act_t, by_h, tasks):
    f, t = act_t.shape
    d = by_h.shape[1]
    rows = f // 8

    def block(i):
        c = place()[2]
        return (i % 4) * 2 + jnp.where(i < 4, 1 - c, c), 0

    def body(i, ins, outs, own):
        mine, theirs, send_sem, recv_sem = own

        def sent(n):
            return pltpu.make_async_remote_copy(
                src_ref=mine.at[n], dst_ref=theirs.at[n], send_sem=send_sem.at[n], recv_sem=recv_sem.at[n],
                device_id=device("c"), device_id_type=pl.DeviceIdType.MESH,
            )

        @pl.when((i >= 1) & (i <= 4))
        def _():
            sent(i - 1).start()

        @pl.when(i < 4)
        def _():
            mine[i] = narrow(dot(ins[0][...], ins[1][...]))

        @pl.when(i >= 4)
        def _():
            new = wide(narrow(dot(ins[0][...], ins[1][...])))
            sent(i - 4).wait()
            outs[0][0] = narrow(new + wide(theirs[i - 4]))

    return line.call(
        "by_down", body, 8, (act_t, by_h), [pl.BlockSpec((rows, t), block), held_block((t, d))],
        (shape(4, rows, d),), [pl.BlockSpec((1, rows, d), lambda i: (jnp.maximum(i - 4, 0), 0, 0))],
        scratch=[
            pltpu.VMEM((4, rows, d), BF16), pltpu.VMEM((4, rows, d), BF16),
            pltpu.SemaphoreType.DMA((4,)), pltpu.SemaphoreType.DMA((4,)),
        ],
        ways=("c",), tasks=tasks, flops=2 * t * d * f,
    )


def move_call(line, tasks):
    def body(i, ins, outs, own):
        outs[0][...] = jnp.zeros_like(outs[0])

    return line.call("move", body, 1, (), [], (shape(8, 128, dtype=F32),), [pl.BlockSpec((8, 128), lambda i: (0, 0))], tasks=tasks)[1]


def second(sums, rx, ry):
    half = sums.shape[1] // 2
    to_y = lax.dynamic_index_in_dim(sums, square_of("y"), 0, False)[:half]
    to_x = lax.dynamic_index_in_dim(sums, square_of("x"), 0, False)[half:]
    return narrow(wide(to_y) + wide(rx[1])), narrow(wide(to_x) + wide(ry[1]))


def whole_block(sums, rx, ry, ry2, rx2):
    half = sums.shape[1] // 2
    own = wide(lax.dynamic_index_in_dim(sums, square_of(), 0, False))
    low = own[:half] + wide(rx[0]) + wide(ry2)
    high = own[half:] + wide(ry[0]) + wide(rx2)
    return narrow(jnp.concatenate([low, high]))


def solution(mesh):
    def step(x, dy, *arrays):
        weights, m, v = (arrays[i : i + 3] for i in (0, 3, 6))
        (wg, wu, wd), line = weights, Line()
        flat = lambda g: g.reshape(-1, g.shape[-1])
        h0, dy = x[0], dy[0]

        (a0, a0t), [[g]] = norm_call(line, h0, [Gather(wg[0])])
        (gate0,), [[u]] = gate_call(line, a0, flat(g), [Gather(wu[0])])
        wg0 = flat(g)
        (up0, act0, act0t), [[d]] = up_call(line, a0, flat(u), gate0, [Gather(wd[0])])
        wu0, wd0 = flat(u), flat(d)
        (h1, a1, a1t), [[g]] = down_call(line, act0, wd0, h0, [Gather(wg[1])])
        wg1 = flat(g)
        (gate1,), [[u]] = gate_call(line, a1, wg1, [Gather(wu[1])])
        wu1 = flat(u)
        (up1, act1, act1t), [[d]] = up_call(line, a1, wu1, gate1, [Gather(wd[1])])
        wd1 = flat(d)

        (sd1,), _ = by_down_call(line, act1t, dy, [])
        (dg1, du1), [pd1] = by_act_call(line, dy, wd1, gate1, up1, [Scatter1(sd1)])
        (sg1,), [qd1] = by_wide_call(line, a1t, dg1, [Scatter2(*second(sd1, *pd1))])
        bd1 = whole_block(sd1, *pd1, *qd1)
        (su1,), [pg1, zd1] = by_wide_call(line, a1t, du1, [Scatter1(sg1), Across(bd1)])
        (da,), [qg1] = by_a_call(line, dg1, wg1, None, [Scatter2(*second(sg1, *pg1))])
        bg1 = whole_block(sg1, *pg1, *qg1)
        (da,), [pu1, zg1] = by_a_call(line, du1, wu1, da, [Scatter1(su1), Across(bg1)])
        by_h = dy + jax.vjp(normed, h1)[1](da)[0]
        (sd0,), [qu1] = by_down_call(line, act0t, by_h, [Scatter2(*second(su1, *pu1))])
        bu1 = whole_block(su1, *pu1, *qu1)
        (dg0, du0), [pd0, zu1] = by_act_call(line, by_h, wd0, gate0, up0, [Scatter1(sd0), Across(bu1)])
        (sg0,), [qd0] = by_wide_call(line, a0t, dg0, [Scatter2(*second(sd0, *pd0))])
        bd0 = whole_block(sd0, *pd0, *qd0)
        (su0,), [pg0, zd0] = by_wide_call(line, a0t, du0, [Scatter1(sg0), Across(bd0)])
        pu0, qg0 = move_call(line, [Scatter1(su0), Scatter2(*second(sg0, *pg0))])
        bg0 = whole_block(sg0, *pg0, *qg0)
        qu0, zg0 = move_call(line, [Scatter2(*second(su0, *pu0)), Across(bg0)])
        bu0 = whole_block(su0, *pu0, *qu0)
        [zu0] = move_call(line, [Across(bu0)])

        total = lambda b, z: wide(narrow(wide(b) + wide(z[0])))
        gradients = [
            jnp.stack([total(bg0, zg0), total(bg1, zg1)]),
            jnp.stack([total(bu0, zu0), total(bu1, zu1)]),
            jnp.stack([total(bd0, zd0), total(bd1, zd1)]),
        ]
        new = [adamw(wide(w), m, v, g) for w, m, v, g in zip(weights, m, v, gradients, strict=True)]
        return tuple(one[which] for which in range(3) for one in new)

    states, cut = P(("rep", "r", "s"), None, None), P(None, "s", None)
    return jax.shard_map(
        step,
        mesh=mesh,
        in_specs=(states, states) + (cut,) * 9,
        out_specs=(P("rep", "s", None),) * 9,
        check_vma=False,
    )
```

time: 1400 us -> 1060 us (0.76)
  Pallas kernels: 0 us -> 926 us
  waiting for transfers between devices: 705 us -> 0 us
  matrix products: 592 us -> 0 us
  other arithmetic: 48.3 us -> 96.6 us
    pallas_call x0 -> x19, Pallas kernels: none -> 926 us  [call(): pl.pallas_call(kernel, grid=(steps,), out_shape=tuple(shapes) + task_shap...]
    dot_general x15 -> x0, matrix products: 592 us -> none  [the longest x5 207 us: layer(): gate = jnp.dot(a, w['w_gate'], preferred_element_type=jnp.float32)]
    reduce_scatter x6 -> x0, waiting for transfers between devices: 291 us -> none  [summed(): lax.psum_scatter(term, 's', scatter_dimension=0, tiled=True)]
    psum x1 -> x0, waiting for transfers between devices: 218 us -> none  [summed(): lax.psum(lax.psum_scatter(term, 's', scatter_dimension=0, tiled=True), 'r')]
    all_gather x6 -> x0, waiting for transfers between devices: 195 us -> none  [fetched(): lax.all_gather(w[number], 's', axis=0, tiled=True)]
    convert_element_type x0 -> x11, other arithmetic: none -> 29.6 us  [the longest x6 17.7 us: narrow(): return value.astype(BF16)]
    another operation x0 -> x11, other arithmetic: none -> 15.3 us
    convert_element_type x2 -> x3, other arithmetic: 32.3 us -> 30.6 us  [adamw(): return ((w - 0.02 * step).astype(jnp.bfloat16), m, v)]
  transfers between devices with their start and end apart: 13 -> 0, of which waited for: 11 -> 0; matrix products, arithmetic and copies ran while one was open for 33% -> 0% of each run, Pallas kernels for 0% -> 0%
where the time goes in v1:
time: 1060 us; the launch traced here: 1050 us
  Pallas kernels  926 us (87%)
  other arithmetic  96.6 us (9%)
  local copies, waits for them, and re-layouts  24.8 us (2%)
    pallas_call x19, Pallas kernels, call(): pl.pallas_call(kernel, grid=(steps,), out_shape=tuple(shapes) + task_shap...  926 us
    convert_element_type x3, other arithmetic, adamw(): return ((w - 0.02 * step).astype(jnp.bfloat16), m, v)  30.6 us

profile of v1, /device:TPU:0, one launch (start us, length us, event | category | flops | bytes accessed | tf_op | source)
XLA Modules:
  0.0 1049.4 jit_solution(7869909848105994398)
XLA Ops:
  0.6 3.7 slice_bitcast_fusion.2
  4.4 61.9 %norm.1 = (bf16[2048,1280]{1,0:T(8,128)(2,1)}, bf16[1280,2048]{1,0:T(8,128)(2,1)}, bf16[8,160,4864]{2,1,0:T(8,128)(2,1)}) custom-call(bf16[2048,1280]{1,0:T(8,128)(2,1)} %bitcast.136, bf16[160,4864]{1,0:T(8,128)(2,1)} %get-tuple-element.299.refs_1_), custom_call_target="tpu_custom_call" | custom-call | tf_op jit(solution)/shard_map/norm/pallas_call | solution.py:216
  66.2 3.7 slice_bitcast_fusion.1
  69.9 61.4 %gate.2 = (f32[2048,4864]{1,0:T(8,128)}, bf16[8,160,4864]{2,1,0:T(8,128)(2,1)}) custom-call(bf16[2048,1280]{1,0:T(8,128)(2,1)} %get-tuple-element.142.refs_0_, bf16[1280,4864]{1,0:T(8,128)(2,1)} %bitcast.140, bf16[160,4864]{1,0:T(8,128)(2,1)} %get-tuple-element.139.refs_2_), custom_call_target="tpu_custom_call" | custom-call | flops 25501368320 | tf_op jit(solution)/shard_map/gate/pallas_call | solution.py:216
  131.3 3.7 slice_bitcast_fusion
  135.0 63.4 %up.2 = (f32[2048,4864]{1,0:T(8,128)}, bf16[2048,4864]{1,0:T(8,128)(2,1)}, bf16[4864,2048]{1,0:T(8,128)(2,1)}, bf16[8,608,1280]{2,1,0:T(8,128)(2,1)}) custom-call(bf16[2048,1280]{1,0:T(8,128)(2,1)} %get-tuple-element.142.refs_0_, bf16[1280,4864]{1,0:T(8,128)(2,1)} %bitcast.145, f32[2048,4864]{1,0:T(8,128)} %get-tuple-element.219.refs_2_, ...), custom_call_target="tpu_custom_call" | custom-call | flops 25501368320 | tf_op jit(solution)/shard_map/up/pallas_call | solution.py:216
  198.4 64.6 %down.1 = (bf16[2048,1280]{1,0:T(8,128)(2,1)}, bf16[2048,1280]{1,0:T(8,128)(2,1)}, bf16[1280,2048]{1,0:T(8,128)(2,1)}, bf16[8,160,4864]{2,1,0:T(8,128)(2,1)}) custom-call(bf16[2048,4864]{1,0:T(8,128)(2,1)} %get-tuple-element.149.refs_0_, bf16[4864,1280]{1,0:T(8,128)(2,1)} %bitcast.133, bf16[2048,1280]{1,0:T(8,128)(2,1)} %bitcast.137, ...), custom_call_target="tpu_custom_call" | custom-call | flops 25501368320 | tf_op jit(solution)/shard_map/down/pallas_call | solution.py:216
  263.1 61.5 %gate.3 = (f32[2048,4864]{1,0:T(8,128)}, bf16[8,160,4864]{2,1,0:T(8,128)(2,1)}) custom-call(bf16[2048,1280]{1,0:T(8,128)(2,1)} %get-tuple-element.161.refs_0_, bf16[1280,4864]{1,0:T(8,128)(2,1)} %bitcast.143, bf16[160,4864]{1,0:T(8,128)(2,1)} %get-tuple-element.158.refs_2_), custom_call_target="tpu_custom_call" | custom-call | flops 25501368320 | tf_op jit(solution)/shard_map/gate/pallas_call | solution.py:216
  324.6 63.2 %up.3 = (f32[2048,4864]{1,0:T(8,128)}, bf16[2048,4864]{1,0:T(8,128)(2,1)}, bf16[4864,2048]{1,0:T(8,128)(2,1)}, bf16[8,608,1280]{2,1,0:T(8,128)(2,1)}) custom-call(bf16[2048,1280]{1,0:T(8,128)(2,1)} %get-tuple-element.161.refs_0_, bf16[1280,4864]{1,0:T(8,128)(2,1)} %bitcast.141, f32[2048,4864]{1,0:T(8,128)} %get-tuple-element.172.refs_2_, ...), custom_call_target="tpu_custom_call" | custom-call | flops 25501368320 | tf_op jit(solution)/shard_map/up/pallas_call | solution.py:216
  387.9 34.4 %by_down.2.refs_4_ = bf16[4,608,1280]{2,1,0:T(8,128)(2,1)} custom-call(bf16[4864,2048]{1,0:T(8,128)(2,1)} %get-tuple-element.168.refs_0_, bf16[2048,1280]{1,0:T(8,128)(2,1)} %bitcast.129), custom_call_target="tpu_custom_call" | custom-call | flops 25501368320 | tf_op jit(solution)/shard_map/by_down/pallas_call | solution.py:216
  422.3 61.8 %by_act.2 = (bf16[2048,4864]{1,0:T(8,128)(2,1)}, bf16[2048,4864]{1,0:T(8,128)(2,1)}, bf16[2,304,1280]{2,1,0:T(8,128)(2,1)}, bf16[2,304,1280]{2,1,0:T(8,128)(2,1)}) custom-call(bf16[2048,1280]{1,0:T(8,128)(2,1)} %bitcast.130, bf16[4864,1280]{1,0:T(8,128)(2,1)} %bitcast.135, f32[2048,4864]{1,0:T(8,128)} %get-tuple-element.172.refs_2_, ...), custom_call_target="tpu_custom_call" | custom-call | flops 25501368320 | tf_op jit(solution)/shard_map/by_act/pallas_call | solution.py:216
  484.2 3.3 fusion.63
  487.5 38.0 %by_wide.4 = (bf16[4,160,4864]{2,1,0:T(8,128)(2,1)}, bf16[304,1280]{1,0:T(8,128)(2,1)}, bf16[304,1280]{1,0:T(8,128)(2,1)}) custom-call(bf16[1280,2048]{1,0:T(8,128)(2,1)} %get-tuple-element.187.refs_0_, bf16[2048,4864]{1,0:T(8,128)(2,1)} %get-tuple-element.194.refs_1_.refs_0_, bf16[304,1280]{1,0:T(8,128)(2,1)} %get-tuple-element.182.refs_2_, ...), custom_call_target="tpu_custom_call" | custom-call | flops 25501368320 | tf_op jit(solution)/shard_map/by_wide/pallas_call | solution.py:216
  525.5 1.8 dynamic-slice_convert_fusion.5
  529.7 1.2 pad_maximum_fusion.3.refs_3_
  530.9 41.0 %by_wide.5 = (bf16[4,160,4864]{2,1,0:T(8,128)(2,1)}, bf16[2,80,4864]{2,1,0:T(8,128)(2,1)}, bf16[2,80,4864]{2,1,0:T(8,128)(2,1)}, bf16[608,1280]{1,0:T(8,128)(2,1)}) custom-call(bf16[1280,2048]{1,0:T(8,128)(2,1)} %get-tuple-element.187.refs_0_, bf16[2048,4864]{1,0:T(8,128)(2,1)} %get-tuple-element.201.refs_1_.refs_0_, ...), custom_call_target="tpu_custom_call" | custom-call | flops 25501368320 | tf_op jit(solution)/shard_map/by_wide/pallas_call | solution.py:216
  571.9 3.3 fusion.65
  575.2 34.7 %by_a.2 = (bf16[2048,1280]{1,0:T(8,128)(2,1)}, bf16[80,4864]{1,0:T(8,128)(2,1)}, bf16[80,4864]{1,0:T(8,128)(2,1)}) custom-call(bf16[2048,4864]{1,0:T(8,128)(2,1)} %get-tuple-element.194.refs_1_.refs_0_, bf16[1280,4864]{1,0:T(8,128)(2,1)} %bitcast.144, bf16[80,4864]{1,0:T(8,128)(2,1)} %get-tuple-element.196.refs_2_, bf16[80,4864]{1,0:T(8,128)(2,1)} %get-tuple-element.197.refs_3_), custom_call_target="tpu_custom_call" | custom-call | flops 25501368320 | tf_op jit(solution)/shard_map/by_a/pallas_call | solution.py:216
  610.0 1.8 dynamic-slice_convert_fusion.4
  614.1 1.2 pad_maximum_fusion.4.refs_4_
  615.4 41.7 %by_a.3 = (bf16[2048,1280]{1,0:T(8,128)(2,1)}, bf16[2,80,4864]{2,1,0:T(8,128)(2,1)}, bf16[2,80,4864]{2,1,0:T(8,128)(2,1)}, bf16[160,4864]{1,0:T(8,128)(2,1)}) custom-call(bf16[2048,4864]{1,0:T(8,128)(2,1)} %get-tuple-element.201.refs_1_.refs_0_, bf16[1280,4864]{1,0:T(8,128)(2,1)} %bitcast.142, bf16[2048,1280]{1,0:T(8,128)(2,1)} %get-tuple-element.203.refs_2_, ...), custom_call_target="tpu_custom_call" | custom-call | flops 25501368320 | tf_op jit(solution)/shard_map/by_a/pallas_call | solution.py:216
  657.1 3.3 fusion.67
  660.4 6.3 fusion.2
  667.6 7.1 fusion.19.refs_1_.refs_0_
  674.7 35.1 %by_down.3 = (bf16[4,608,1280]{2,1,0:T(8,128)(2,1)}, bf16[80,4864]{1,0:T(8,128)(2,1)}, bf16[80,4864]{1,0:T(8,128)(2,1)}) custom-call(bf16[4864,2048]{1,0:T(8,128)(2,1)} %get-tuple-element.210.refs_0_, bf16[2048,1280]{1,0:T(8,128)(2,1)} %fusion.19.refs_1_.refs_0_, bf16[80,4864]{1,0:T(8,128)(2,1)} %get-tuple-element.212.refs_2_, ...), custom_call_target="tpu_custom_call" | custom-call | flops 25501368320 | tf_op jit(solution)/shard_map/by_down/pallas_call | solution.py:216
  709.8 1.8 dynamic-slice_convert_fusion.3
  715.2 61.4 %by_act.3 = (bf16[2048,4864]{1,0:T(8,128)(2,1)}, bf16[2048,4864]{1,0:T(8,128)(2,1)}, bf16[2,304,1280]{2,1,0:T(8,128)(2,1)}, bf16[2,304,1280]{2,1,0:T(8,128)(2,1)}, bf16[160,4864]{1,0:T(8,128)(2,1)}) custom-call(bf16[2048,1280]{1,0:T(8,128)(2,1)} %fusion.19.refs_1_.refs_0_, bf16[4864,1280]{1,0:T(8,128)(2,1)} %bitcast.134, ...), custom_call_target="tpu_custom_call" | custom-call | flops 25501368320 | tf_op jit(solution)/shard_map/by_act/pallas_call | solution.py:216
  776.6 3.3 fusion.69
  780.0 38.4 %by_wide.6 = (bf16[4,160,4864]{2,1,0:T(8,128)(2,1)}, bf16[304,1280]{1,0:T(8,128)(2,1)}, bf16[304,1280]{1,0:T(8,128)(2,1)}) custom-call(bf16[1280,2048]{1,0:T(8,128)(2,1)} %get-tuple-element.234.refs_0_, bf16[2048,4864]{1,0:T(8,128)(2,1)} %get-tuple-element.227.refs_1_, bf16[304,1280]{1,0:T(8,128)(2,1)} %get-tuple-element.228.refs_2_, ...), custom_call_target="tpu_custom_call" | custom-call | flops 25501368320 | tf_op jit(solution)/shard_map/by_wide/pallas_call | solution.py:216
  818.4 1.8 dynamic-slice_convert_fusion.1
  821.7 1.3 pad_maximum_fusion.6.refs_3_
  823.3 40.6 %by_wide.7 = (bf16[4,160,4864]{2,1,0:T(8,128)(2,1)}, bf16[2,80,4864]{2,1,0:T(8,128)(2,1)}, bf16[2,80,4864]{2,1,0:T(8,128)(2,1)}, bf16[608,1280]{1,0:T(8,128)(2,1)}) custom-call(bf16[1280,2048]{1,0:T(8,128)(2,1)} %get-tuple-element.234.refs_0_, bf16[2048,4864]{1,0:T(8,128)(2,1)} %get-tuple-element.235.refs_1_, ...), custom_call_target="tpu_custom_call" | custom-call | flops 25501368320 | tf_op jit(solution)/shard_map/by_wide/pallas_call | solution.py:216
  863.9 3.3 fusion.24
  867.2 10.3 fusion.14
  877.6 4.8 dynamic-slice_convert_fusion
  882.4 1.5 fusion.71
  883.9 53.0 %move.3 = (f32[8,128]{1,0:T(8,128)}, bf16[2,80,4864]{2,1,0:T(8,128)(2,1)}, bf16[2,80,4864]{2,1,0:T(8,128)(2,1)}, bf16[80,4864]{1,0:T(8,128)(2,1)}, bf16[80,4864]{1,0:T(8,128)(2,1)}) custom-call(bf16[4,160,4864]{2,1,0:T(8,128)(2,1)} %get-tuple-element.241.refs_0_, bf16[80,4864]{1,0:T(8,128)(2,1)} %get-tuple-element.242.refs_1_, ...), custom_call_target="tpu_custom_call" | custom-call | tf_op jit(solution)/shard_map/move/pallas_call | solution.py:216
  936.9 3.2 fusion.43
  940.1 1.2 pad_maximum_fusion.7.refs_2_
  942.8 2.9 fusion.73
  945.7 35.5 %move.4 = (f32[8,128]{1,0:T(8,128)}, bf16[80,4864]{1,0:T(8,128)(2,1)}, bf16[80,4864]{1,0:T(8,128)(2,1)}, bf16[160,4864]{1,0:T(8,128)(2,1)}) custom-call(bf16[80,4864]{1,0:T(8,128)(2,1)} %get-tuple-element.248.refs_0_, bf16[80,4864]{1,0:T(8,128)(2,1)} %get-tuple-element.249.refs_1_, bf16[160,4864]{1,0:T(8,128)(2,1)} %pad_maximum_fusion.7.refs_2_), custom_call_target="tpu_custom_call" | custom-call | tf_op jit(solution)/shard_map/move/pallas_call | solution.py:216
  981.2 3.2 fusion.31
  985.6 1.2 pad_maximum_fusion.8.refs_0_
  986.8 34.7 %move.5 = (f32[8,128]{1,0:T(8,128)}, bf16[160,4864]{1,0:T(8,128)(2,1)}) custom-call(bf16[160,4864]{1,0:T(8,128)(2,1)} %pad_maximum_fusion.8.refs_0_), custom_call_target="tpu_custom_call" | custom-call | tf_op jit(solution)/shard_map/move/pallas_call | solution.py:216
  1021.5 2.3 fusion.22
  1024.3 1.5 copy-done.2
  1025.7 10.2 fusion.10
  1038.9 10.1 fusion.6
  (104 shorter events, 16.7 us)
Async XLA Ops:
  525.5 1.9 copy-start.21
  525.5 2.3 copy-start.22
  525.5 2.5 copy-start.35
  525.5 2.7 copy-start.36
  528.8 0.9 copy-start.8
  528.8 2.1 copy-start.10
  610.0 1.9 copy-start.33
  610.0 2.3 copy-start.34
  610.0 2.5 copy-start.37
  610.0 2.7 copy-start.38
  613.2 0.9 copy-start.4
  613.2 2.1 copy-start.6
  660.4 6.4 slice-start
  660.4 6.4 slice-start.1
  660.4 7.1 copy-start
  709.8 1.9 copy-start.27
  709.8 2.3 copy-start.28
  709.8 2.5 copy-start.39
  709.8 2.7 copy-start.40
  713.1 0.9 copy-start.12
  818.3 1.9 copy-start.31
  818.3 2.3 copy-start.32
  818.4 2.5 copy-start.41
  818.4 2.7 copy-start.42
  821.6 1.4 copy-start.16
  821.7 1.6 copy-start.17
  823.3 40.6 %copy-start.9 = (bf16[304,1280]{1,0:T(8,128)(2,1)S(1)}, bf16[304,1280]{1,0:T(8,128)(2,1)}, u32[]{:S(2)}) copy-start(bf16[304,1280]{1,0:T(8,128)(2,1)} %copy-done.8) | copy-start | bytes 2334724
  823.3 40.6 %copy-start.11 = (bf16[304,1280]{1,0:T(8,128)(2,1)S(1)}, bf16[304,1280]{1,0:T(8,128)(2,1)}, u32[]{:S(2)}) copy-start(bf16[304,1280]{1,0:T(8,128)(2,1)} %copy-done.10) | copy-start | bytes 2334724
  863.9 3.3 copy-start.1
  863.9 13.6 %slice-start.2 = ((s8[6225920]{0:T(1024)(128)(4,1)}), s8[4194304]{0:T(1024)(128)(4,1)S(1)}, s32[]{:S(2)}) async-start(s8[6225920]{0:T(1024)(128)(4,1)} %bitcast.138), calls=%async_computation.2 | async-start | bytes 8388608
  867.2 10.3 slice-start.3
  877.6 4.8 copy-start.24
  877.6 4.8 copy-start.25
  940.1 5.6 copy-start.14
  940.1 2.2 copy-start.29
  940.1 2.7 copy-start.30
  984.4 0.9 copy-start.18
  984.5 1.1 copy-start.19
  986.8 37.0 %copy-start.13 = (bf16[80,4864]{1,0:T(8,128)(2,1)S(1)}, bf16[80,4864]{1,0:T(8,128)(2,1)}, u32[]{:S(2)}) copy-start(bf16[80,4864]{1,0:T(8,128)(2,1)} %copy-done.12) | copy-start | bytes 2334724
  1021.5 2.3 copy-start.23
  1023.8 1.9 copy-start.2
  1025.7 10.2 copy-start.15
  1025.7 10.3 copy-start.26
  1036.0 1.1 copy-start.5
  1036.0 1.4 copy-start.7
  1036.0 1.9 copy-start.20
  1036.4 2.5 copy-start.3

commit v2 on v1

v2 whole, which is shorter than its diff:
```python
import functools

import jax
import jax.numpy as jnp
from jax import lax
from jax.experimental import pallas as pl
from jax.experimental.pallas import tpu as pltpu
from jax.sharding import PartitionSpec as P

BF16, F32 = jnp.bfloat16, jnp.float32
LIMIT = 61 * 1024 * 1024
ANY = pl.BlockSpec(memory_space=pl.ANY)


def normed(h):
    wide = h.astype(jnp.float32)
    scale = lax.rsqrt(jnp.mean(wide**2, -1, keepdims=True) + 1e-6)
    return (wide * scale).astype(jnp.bfloat16)


def by_norm(h, by):
    h, by = h.astype(jnp.float32), by.astype(jnp.float32)
    scale = lax.rsqrt(jnp.mean(h**2, -1, keepdims=True) + 1e-6)
    return (by * scale - h * (scale**3 * jnp.mean(by * h, -1, keepdims=True))).astype(jnp.bfloat16)


def adamw(w, m, v, g):
    m = 0.9 * m + 0.1 * g
    v = 0.95 * v + 0.05 * g * g
    step = m * lax.rsqrt(v + 1e-8) + 0.1 * w
    return (w - 0.02 * step).astype(jnp.bfloat16), m, v


def wide(value):
    return value.astype(F32)


def narrow(value):
    return value.astype(BF16)


def place():
    me = lax.axis_index("s")
    return me // 4, (me // 2) % 2, me % 2


def index_of(*changed):
    x, y, c = place()
    x, y, c = (1 - v if k in changed else v for k, v in (("x", x), ("y", y), ("c", c)))
    return x * 4 + y * 2 + c


def square_of(*changed):
    x, y, _ = place()
    x, y = (1 - v if k in changed else v for k, v in (("x", x), ("y", y)))
    return x * 2 + y


def device(way):
    return {"r": 1 - lax.axis_index("r")} if way == "z" else {"s": index_of(way)}


class Sends:
    def __init__(self, send_sem, recv_sem, scratch):
        self.send_sem, self.recv_sem, self.scratch = send_sem, recv_sem, scratch

    def copy(self, number, way, src, dst):
        return pltpu.make_async_remote_copy(
            src_ref=src, dst_ref=dst, send_sem=self.send_sem.at[number], recv_sem=self.recv_sem.at[number],
            device_id=device(way), device_id_type=pl.DeviceIdType.MESH,
        )


class Gather1:
    ways, copies, when, alias, held, scratch = ("x", "y", "c"), 3, (), {}, True, ()

    def __init__(self, blocks, number):
        self.operands = (blocks,)
        self.spec = pl.BlockSpec((1,) + blocks.shape[1:], lambda i: (number, 0, 0), pipeline_mode=pl.Buffered(1))
        self.shapes = (jax.ShapeDtypeStruct((8,) + blocks.shape[1:], blocks.dtype),)
        self.quarter = blocks.shape[1] // 4

    def stage(self, number, sends, ins, outs, local):
        b, g = ins[0].at[0], outs[0]
        me, part = index_of(), pl.ds(lax.axis_index("r") * self.quarter, 3 * self.quarter)
        own = pltpu.make_async_copy(b, g.at[me], local)
        copies = [sends.copy(0, "x", b.at[part], g.at[me, part]), sends.copy(1, "y", b.at[part], g.at[me, part]), sends.copy(2, "c", b, g.at[me])]
        for each in copies + [own]:
            each.start() if number == 0 else each.wait()


class Gather2:
    ways, copies, when, alias = ("x", "y", "z", "c"), 11, (0.5,), {0: 0}
    held, scratch = False, ()

    def __init__(self, so_far):
        self.operands = (so_far,)
        self.shapes = (jax.ShapeDtypeStruct(so_far.shape, so_far.dtype),)
        self.quarter = so_far.shape[1] // 4

    def stage(self, number, sends, ins, outs, local):
        g, q, z = outs[0], self.quarter, lax.axis_index("r")
        by_x, by_y, far = index_of("x"), index_of("y"), index_of("x", "y")
        three, theirs, missing = pl.ds(z * q, 3 * q), pl.ds(z * 3 * q, q), pl.ds((1 - z) * 3 * q, q)
        first, second = pl.ds(z * 2 * q, q), pl.ds(z * 2 * q + q, q)
        near, other = pl.ds(z * 2 * q, 2 * q), pl.ds((1 - z) * 2 * q, 2 * q)
        copies = [
            ("y", by_x, first), ("x", by_y, second), ("z", by_x, theirs), ("z", by_y, theirs), ("c", by_x, three), ("c", by_y, three),
            ("z", far, near), ("c", far, near), ("c", by_x, missing), ("c", by_y, missing), ("c", far, other),
        ]
        part = [sends.copy(n, way, g.at[block, rows], g.at[block, rows]) for n, (way, block, rows) in enumerate(copies)]
        if number == 0:
            for each in part[:6]:
                each.start()
        elif number == 1:
            part[0].wait_recv()
            part[1].wait_recv()
            part[6].start()
            part[7].start()
        else:
            part[2].wait_recv()
            part[8].start()
            part[3].wait_recv()
            part[9].start()
            part[6].wait_recv()
            part[10].start()
            for each in (4, 5, 7, 8, 9, 10):
                part[each].wait_recv()
            for each in part:
                each.wait_send()


class Hops:
    when, alias, held = (), {}, False

    def __init__(self, *sent):
        self.ways, self.operands = zip(*sent)
        self.copies, self.scratch = len(sent), ()
        self.shapes = tuple(jax.ShapeDtypeStruct(v.shape, v.dtype) for v in self.operands)

    def stage(self, number, sends, ins, outs, local):
        for n, way in enumerate(self.ways):
            each = sends.copy(n, way, ins[n], outs[n])
            each.start() if number == 0 else each.wait()


class LastHops:
    ways, alias, held, start, piece = ("x", "y", "z"), {}, False, 8, 64

    def __init__(self, to_y, to_x, part):
        self.pieces = [(at, min(self.piece, part.shape[0] - at)) for at in range(0, part.shape[0], self.piece)]
        self.copies = 2 + len(self.pieces)
        self.when = tuple(range(self.start, self.start + 1 + len(self.pieces)))
        self.operands = (to_y, to_x, part)
        self.half = to_y.shape[0]
        self.shapes = (jax.ShapeDtypeStruct(part.shape, BF16),) * 2
        hop = pltpu.VMEM(to_y.shape, BF16)
        self.scratch = (hop, hop, pltpu.VMEM(part.shape, F32), pltpu.VMEM(part.shape, BF16), pltpu.SemaphoreType.DMA)

    def stage(self, number, sends, ins, outs, local):
        (to_y, to_x, part), (block, over), (*scratch, out_sem) = ins, outs, sends.scratch
        from_y, from_x, sums, total = scratch
        low, high = pl.ds(0, self.half), pl.ds(self.half, self.half)
        by_y, by_x = sends.copy(0, "y", to_y, from_y), sends.copy(1, "x", to_x, from_x)
        across = [sends.copy(2 + n, "z", total.at[pl.ds(*piece)], over.at[pl.ds(*piece)]) for n, piece in enumerate(self.pieces)]
        load, store = pltpu.make_async_copy(part, sums, local), pltpu.make_async_copy(total, block, out_sem)
        if number == 0:
            for each in (by_y, by_x, load):
                each.start()
        elif number == 1:
            for each in (by_y, by_x, load):
                each.wait()
            total[low] = narrow(sums[low] + wide(from_y[...]))
            total[high] = narrow(sums[high] + wide(from_x[...]))
        elif number < 2 + len(across):
            across[number - 2].start()
            if number == 2:
                store.start()
        else:
            for each in across + [store]:
                each.wait()


class Line:
    def __init__(self):
        self.calls, self.last = 0, None

    def call(self, name, body, steps, operands, in_specs, shapes, out_specs, scratch=(), ways=(), tasks=(), flops=0):
        tasks = list(tasks)
        ways = tuple(sorted(set(ways).union(*(t.ways for t in tasks))))
        counts = [len(operands), sum(len(t.operands) for t in tasks), len(shapes), sum(len(t.shapes) for t in tasks), len(scratch)]

        def kernel(*refs):
            refs = list(refs)
            ins, task_ins, outs, task_outs, own = ([refs.pop(0) for _ in range(n)] for n in counts)
            i = pl.program_id(0)
            held = []
            for t in tasks:
                a, task_ins = task_ins[: len(t.operands)], task_ins[len(t.operands) :]
                b, task_outs = task_outs[: len(t.shapes)], task_outs[len(t.shapes) :]
                sems, more, refs = refs[:3], refs[3 : 3 + len(t.scratch)], refs[3 + len(t.scratch) :]
                held.append((t, Sends(sems[0], sems[1], more), a, b, sems[2]))

            if ways:
                @pl.when(i == 0)
                def _():
                    barrier = pltpu.get_barrier_semaphore()
                    for way in ways:
                        pl.semaphore_signal(barrier, inc=1, device_id=device(way), device_id_type=pl.DeviceIdType.MESH)
                    pl.semaphore_wait(barrier, len(ways))
                    for t, sends, a, b, local in held:
                        t.stage(0, sends, a, b, local)

            for t, sends, a, b, local in held:
                for number, when in enumerate(t.when):
                    @pl.when(i == (when if isinstance(when, int) else int(steps * when)))
                    def _():
                        t.stage(number + 1, sends, a, b, local)

            if body is not None:
                body(i, ins, outs, own)

            if held:
                @pl.when(i == steps - 1)
                def _():
                    for t, sends, a, b, local in held:
                        t.stage(len(t.when) + 1, sends, a, b, local)

        sems = []
        for t in tasks:
            sems += [pltpu.SemaphoreType.DMA((t.copies,)), pltpu.SemaphoreType.DMA((t.copies,)), pltpu.SemaphoreType.DMA, *t.scratch]
        task_operands = tuple(o for t in tasks for o in t.operands)
        task_shapes = tuple(s for t in tasks for s in t.shapes)
        given = tuple(operands) + task_operands
        if self.last is not None:
            given, _ = lax.optimization_barrier((given, self.last))
        aliases, ins, outs = {}, len(operands), len(shapes)
        for t in tasks:
            aliases.update({ins + a: outs + b for a, b in t.alias.items()})
            ins, outs = ins + len(t.operands), outs + len(t.shapes)
        params = {"collective_id": self.calls, "has_side_effects": True} if ways else {}
        results = pl.pallas_call(
            kernel,
            grid=(steps,),
            out_shape=tuple(shapes) + task_shapes,
            in_specs=list(in_specs) + [t.spec if t.held else ANY for t in tasks for o in t.operands],
            out_specs=list(out_specs) + [ANY] * len(task_shapes),
            scratch_shapes=list(scratch) + sems,
            name=name,
            input_output_aliases=aliases,
            compiler_params=pltpu.CompilerParams(dimension_semantics=("arbitrary",), vmem_limit_bytes=LIMIT, **params),
            cost_estimate=pl.CostEstimate(flops=flops, bytes_accessed=0, transcendentals=0),
        )(*given)
        self.calls += 1
        self.last = results[0]
        own, rest = results[: len(shapes)], list(results[len(shapes) :])
        moved = [[rest.pop(0) for _ in t.shapes] for t in tasks]
        return own, moved


def shape(*dims, dtype=BF16):
    return jax.ShapeDtypeStruct(dims, dtype)


def held_block(dims):
    return pl.BlockSpec(dims, lambda i: (0,) * len(dims), pipeline_mode=pl.Buffered(1))


def dot(a, b, contract=(1, 0)):
    return lax.dot_general(a, b, (((contract[0],), (contract[1],)), ((), ())), preferred_element_type=F32)


WIDTH = 256
TALL = 256


def norm_call(line, h, tasks):
    t, d = h.shape

    def body(i, ins, outs, own):
        a = normed(ins[0][...])
        outs[0][...] = a
        outs[1][...] = a.T

    return line.call(
        "norm", body, t // TALL, (h,), [pl.BlockSpec((TALL, d), lambda i: (i, 0))], (shape(t, d), shape(d, t)),
        [pl.BlockSpec((TALL, d), lambda i: (i, 0)), pl.BlockSpec((d, TALL), lambda i: (0, i))], tasks=tasks,
    )


def gate_call(line, a, w, tasks):
    t, d = a.shape
    f = w.shape[1]

    def body(i, ins, outs, own):
        outs[0][...] = dot(ins[0][...], ins[1][...])

    return line.call(
        "gate", body, f // WIDTH, (a, w), [held_block((t, d)), pl.BlockSpec((d, WIDTH), lambda i: (0, i))],
        (shape(t, f, dtype=F32),), [pl.BlockSpec((t, WIDTH), lambda i: (0, i))], tasks=tasks, flops=2 * t * d * f,
    )


def up_call(line, a, w, gate, tasks):
    t, d = a.shape
    f = w.shape[1]
    rows = lambda n: pl.BlockSpec((TALL, n), lambda i: (i, 0))

    def body(i, ins, outs, own):
        for start in range(0, f, WIDTH):
            s = slice(start, start + WIDTH)
            up = dot(ins[0][...], ins[1][:, s])
            outs[0][:, s] = up
            act = narrow(jax.nn.silu(ins[2][:, s]) * up)
            outs[1][:, s] = act
            outs[2][s] = act.T

    return line.call(
        "up", body, t // TALL, (a, w, gate), [rows(d), held_block((d, f)), rows(f)],
        (shape(t, f, dtype=F32), shape(t, f), shape(f, t)), [rows(f), rows(f), pl.BlockSpec((f, TALL), lambda i: (0, i))],
        tasks=tasks, flops=2 * t * d * f,
    )


def down_call(line, act, w, h, tasks):
    t, f = act.shape
    d = w.shape[1]
    rows = lambda n: pl.BlockSpec((TALL, n), lambda i: (i, 0))

    def body(i, ins, outs, own):
        new = ins[2][...] + narrow(dot(ins[0][...], ins[1][...]))
        outs[0][...] = new
        a = normed(new)
        outs[1][...] = a
        outs[2][...] = a.T

    return line.call(
        "down", body, t // TALL, (act, w, h), [rows(f), held_block((f, d)), rows(d)], (shape(t, d), shape(t, d), shape(d, t)),
        [rows(d), rows(d), pl.BlockSpec((d, TALL), lambda i: (0, i))], tasks=tasks, flops=2 * t * d * f,
    )


def by_a_call(line, by, w, more, tasks):
    t, f = by.shape
    d = w.shape[0]
    rows = lambda n: pl.BlockSpec((TALL, n), lambda i: (i, 0))

    def body(i, ins, outs, own):
        new = narrow(dot(ins[0][...], ins[1][...], (1, 1)))
        if more:
            new = narrow(wide(new) + wide(ins[2][...]))
            new = ins[4][...] + by_norm(ins[3][...], new)
        outs[0][...] = new

    return line.call(
        "by_a", body, t // TALL, (by, w) + more, [rows(f), held_block((d, f))] + [rows(d)] * len(more), (shape(t, d),), [rows(d)],
        tasks=tasks, flops=2 * t * d * f,
    )


RING = 6
HOPS = 4


def by_hidden_call(line, by_h, w, gate, up, a_t, tasks, first):
    t, d = by_h.shape
    f = w.shape[0]
    rows, half, tiles, both = d // 8, d // 16, f // WIDTH, 2 * WIDTH
    last = tiles - 1
    tile = pl.BlockSpec((t, WIDTH), lambda i: (0, jnp.minimum(i, last)))
    hops = HOPS if first else 2
    at = lambda *dims: pl.BlockSpec(dims, lambda i: (0, jnp.maximum(i - 2 * hops, 0)))
    low, high = pl.ds(0, half), pl.ds(half, half)

    def body(i, ins, outs, own):
        by, mine, theirs, pair, rx, ry, to_y, to_x, ry2, rx2, block, over, *sems = own
        c, here, by_x, by_y, far = place()[2], square_of(), square_of("x"), square_of("y"), square_of("x", "y")

        def copies(hop, n):
            k = n % RING
            made = {
                0: lambda: [("c", mine.at[k, 1 - c], theirs.at[k])],
                1: lambda: [
                    ("x", pair.at[k, far, low], rx.at[k, 1]), ("y", pair.at[k, far, high], ry.at[k, 1]),
                    ("x", pair.at[k, by_x, low], rx.at[k, 0]), ("y", pair.at[k, by_y, high], ry.at[k, 0]),
                ],
                2: lambda: [("y", to_y.at[k], ry2.at[k]), ("x", to_x.at[k], rx2.at[k])],
                3: lambda: [("z", block.at[k], over.at[k])],
            }[hop]()
            return [
                pltpu.make_async_remote_copy(
                    src_ref=src, dst_ref=dst, send_sem=sems[2 * hop].at[k, p], recv_sem=sems[2 * hop + 1].at[k, p],
                    device_id=device(way), device_id_type=pl.DeviceIdType.MESH,
                )
                for p, (way, src, dst) in enumerate(made)
            ]

        for hop in reversed(range(hops)):
            n = i - 1 - 2 * hop

            @pl.when((n >= 0) & (n < tiles))
            def _():
                for each in copies(hop, n):
                    each.start()

        @pl.when(i < tiles)
        def _():
            for start in range(0, t, 256):
                s = slice(start, start + 256)
                by_act = wide(narrow(dot(ins[0][s], ins[1][...], (1, 1))))
                gate = ins[2][s]
                share = jax.nn.sigmoid(gate)
                silu = gate * share
                by_gate = narrow(by_act * ins[3][s] * (share + silu * (1 - share)))
                by_up = narrow(by_act * silu)
                by[s, :WIDTH] = by_gate
                by[s, WIDTH:] = by_up
                if not first:
                    outs[6][s] = by_gate
                    outs[7][s] = by_up
            new = narrow(dot(ins[4][...], by[...])).reshape(4, 2, rows, both)
            mine[i % RING, 0] = new[:, 0]
            mine[i % RING, 1] = new[:, 1]

        def arrived(hop, act):
            n = i - 2 - 2 * hop

            @pl.when((n >= 0) & (n < tiles))
            def _():
                for each in copies(hop, n):
                    each.wait()
                act(n % RING)

        def of_pair(k):
            pair[k] = narrow(wide(mine[k, c]) + wide(theirs[k]))

        def of_first(k):
            if not first:
                for m in (0, 1):
                    s = pl.ds(m * WIDTH, WIDTH)
                    outs[3 * m][...] = narrow(wide(pair[k, by_y, low, s]) + wide(rx[k, 1, :, s]))
                    outs[3 * m + 1][...] = narrow(wide(pair[k, by_x, high, s]) + wide(ry[k, 1, :, s]))
                    outs[3 * m + 2][low] = wide(pair[k, here, low, s]) + wide(rx[k, 0, :, s])
                    outs[3 * m + 2][high] = wide(pair[k, here, high, s]) + wide(ry[k, 0, :, s])
                return
            to_y[k] = narrow(wide(pair[k, by_y, low]) + wide(rx[k, 1]))
            to_x[k] = narrow(wide(pair[k, by_x, high]) + wide(ry[k, 1]))

        def of_second(k):
            block[k, low] = narrow(wide(pair[k, here, low]) + wide(rx[k, 0]) + wide(ry2[k]))
            block[k, high] = narrow(wide(pair[k, here, high]) + wide(ry[k, 0]) + wide(rx2[k]))

        def of_all(k):
            total = narrow(wide(block[k]) + wide(over[k]))
            outs[0][...] = total[:, :WIDTH]
            outs[1][...] = total[:, WIDTH:]

        for hop, act in enumerate((of_pair, of_first, of_second, of_all)[:hops]):
            arrived(hop, act)

    if first:
        shapes, out_specs = (shape(rows, f),) * 2, [at(rows, WIDTH)] * 2
    else:
        shapes = (shape(half, f), shape(half, f), shape(rows, f, dtype=F32)) * 2 + (shape(t, f),) * 2
        out_specs = [at(half, WIDTH), at(half, WIDTH), at(rows, WIDTH)] * 2 + [tile, tile]
    return line.call(
        "by_hidden", body, tiles + 2 * hops, (by_h, w, gate, up, a_t),
        [held_block((t, d)), pl.BlockSpec((WIDTH, d), lambda i: (jnp.minimum(i, last), 0)), tile, tile, held_block((d, t))],
        shapes, out_specs,
        scratch=[
            pltpu.VMEM((t, both), BF16),
            pltpu.VMEM((RING, 2, 4, rows, both), BF16), pltpu.VMEM((RING, 4, rows, both), BF16), pltpu.VMEM((RING, 4, rows, both), BF16),
            pltpu.VMEM((RING, 2, half, both), BF16), pltpu.VMEM((RING, 2, half, both), BF16),
            *[pltpu.VMEM((RING, half, both), BF16)] * 4, *[pltpu.VMEM((RING, rows, both), BF16)] * 2,
            *[pltpu.SemaphoreType.DMA((RING, n)) for n in (1, 1, 4, 4, 2, 2, 1, 1)],
        ],
        ways=("c", "x", "y", "z") if first else ("c", "x", "y"), tasks=tasks, flops=6 * t * d * f,
    )


def by_down_call(line, act_t, by_h, tasks):
    f, t = act_t.shape
    d = by_h.shape[1]
    rows = f // 8
    half = rows // 2
    low, high = pl.ds(0, half), pl.ds(half, half)

    def block(i):
        x, y, c = place()
        n = i // 2
        there_x = jnp.where(n % 2 == 0, jnp.where(n == 0, 1 - x, x), jnp.where(n == 1, 1 - x, x))
        there_y = jnp.where(n % 2 == 0, 1 - y, y)
        return (there_x * 2 + there_y) * 2 + jnp.where(i % 2 == 0, 1 - c, c), 0

    def body(i, ins, outs, own):
        mine, theirs, pair, send_sem, recv_sem, hop_send, hop_recv = own
        rx, ry = outs[1:]

        def remote(way, src, dst, send, recv):
            return pltpu.make_async_remote_copy(
                src_ref=src, dst_ref=dst, send_sem=send, recv_sem=recv, device_id=device(way), device_id_type=pl.DeviceIdType.MESH,
            )

        def sent(n):
            return remote("c", mine.at[n], theirs.at[n], send_sem.at[n], recv_sem.at[n])

        made = [("x", 0, low, rx.at[1]), ("y", 0, high, ry.at[1]), ("x", 1, low, rx.at[0]), ("y", 2, high, ry.at[0])]
        hop = [remote(way, pair.at[n, part], dst, hop_send.at[p], hop_recv.at[p]) for p, (way, n, part, dst) in enumerate(made)]

        @pl.when(i % 2 == 1)
        def _():
            sent(i // 2).start()

        for step, copies in ((2, hop[:2]), (4, hop[2:3]), (6, hop[3:])):
            @pl.when(i == step)
            def _():
                for each in copies:
                    each.start()

        @pl.when(i % 2 == 0)
        def _():
            mine[i // 2] = narrow(dot(ins[0][...], ins[1][...]))

        @pl.when(i % 2 == 1)
        def _():
            new = wide(narrow(dot(ins[0][...], ins[1][...])))
            n = i // 2
            sent(n).wait()
            total = narrow(new + wide(theirs[n]))
            pair[n] = total
            outs[0][0] = total

        @pl.when(i == 7)
        def _():
            for each in hop:
                each.wait()

    hopped = shape(2, half, d)
    return line.call(
        "by_down", body, 8, (act_t, by_h), [pl.BlockSpec((rows, t), block), held_block((t, d))],
        (shape(4, rows, d), hopped, hopped), [pl.BlockSpec((1, rows, d), lambda i: (i // 2, 0, 0)), ANY, ANY],
        scratch=[
            *[pltpu.VMEM((4, rows, d), BF16)] * 3,
            *[pltpu.SemaphoreType.DMA((4,))] * 4,
        ],
        ways=("c", "x", "y"), tasks=tasks, flops=2 * t * d * f,
    )


def move_call(line, tasks):
    def body(i, ins, outs, own):
        outs[0][...] = jnp.zeros_like(outs[0])

    return line.call("move", body, 1, (), [], (shape(8, 128, dtype=F32),), [pl.BlockSpec((8, 128), lambda i: (0, 0))], tasks=tasks)[1]


def second(sums, rx, ry):
    half = sums.shape[1] // 2
    to_y, to_x = wide(sums[2, :half]) + wide(rx[1]), wide(sums[1, half:]) + wide(ry[1])
    return narrow(to_y), narrow(to_x), wide(sums[3]) + wide(jnp.concatenate([rx[0], ry[0]]))


def solution(mesh):
    def step(x, dy, *arrays):
        weights, m, v = (arrays[i : i + 3] for i in (0, 3, 6))
        (wg, wu, wd), line = weights, Line()
        flat = lambda g: g.reshape(-1, g.shape[-1])
        h0, dy = x[0], dy[0]

        (a0, a0t), [[g]] = norm_call(line, h0, [Gather1(wg, 0)])
        [wg0], [u] = move_call(line, [Gather2(g), Gather1(wu, 0)])
        wg0 = flat(wg0)
        (gate0,), [[wu0], [d]] = gate_call(line, a0, wg0, [Gather2(u), Gather1(wd, 0)])
        wu0 = flat(wu0)
        (up0, act0, act0t), [[wd0], [g]] = up_call(line, a0, wu0, gate0, [Gather2(d), Gather1(wg, 1)])
        wd0 = flat(wd0)
        (h1, a1, a1t), [[wg1], [u]] = down_call(line, act0, wd0, h0, [Gather2(g), Gather1(wu, 1)])
        wg1 = flat(wg1)
        (gate1,), [[wu1], [d]] = gate_call(line, a1, wg1, [Gather2(u), Gather1(wd, 1)])
        wu1 = flat(wu1)
        (up1, act1, act1t), [[wd1]] = up_call(line, a1, wu1, gate1, [Gather2(d)])
        wd1 = flat(wd1)

        down1, _ = by_down_call(line, act1t, dy, [])
        to_y, to_x, part = second(*down1)
        (gy, gx, gpart, uy, ux, upart, dg1, du1), [(from_y, from_x)] = by_hidden_call(
            line, dy, wd1, gate1, up1, a1t, [Hops(("y", to_y), ("x", to_x))], False
        )
        joined = lambda part, from_y, from_x: narrow(part + wide(jnp.concatenate([from_y, from_x])))
        bd1 = joined(part, from_y, from_x)
        (da,), [(gfy, gfx, ufy, ufx), (zd1,)] = by_a_call(
            line, dg1, wg1, (), [Hops(("y", gy), ("x", gx), ("y", uy), ("x", ux)), Hops(("z", bd1))]
        )
        bg1, bu1 = joined(gpart, gfy, gfx), joined(upart, ufy, ufx)
        (by_h,), [(zg1,)] = by_a_call(line, du1, wu1, (da, h1, dy), [Hops(("z", bg1))])
        down0, [(zu1,)] = by_down_call(line, act0t, by_h, [Hops(("z", bu1))])
        (g0, u0), [(bd0, zd0)] = by_hidden_call(line, by_h, wd0, gate0, up0, a0t, [LastHops(*second(*down0))], True)

        total = lambda b, z: narrow(wide(b) + wide(z))
        gradients = [
            wide(jnp.stack(pair))
            for pair in ([g0, total(bg1, zg1)], [u0, total(bu1, zu1)], [total(bd0, zd0), total(bd1, zd1)])
        ]
        new = [adamw(wide(w), m, v, g) for w, m, v, g in zip(weights, m, v, gradients, strict=True)]
        return tuple(one[which] for which in range(3) for one in new)

    states, cut = P(("rep", "r", "s"), None, None), P(None, "s", None)
    return jax.shard_map(
        step,
        mesh=mesh,
        in_specs=(states, states) + (cut,) * 9,
        out_specs=(P("rep", "s", None),) * 9,
        check_vma=False,
    )
```

time: 1060 us -> 829 us (0.78)
  Pallas kernels: 926 us -> 755 us
  other arithmetic: 96.6 us -> 58.1 us
  local copies, waits for them, and re-layouts: 24.8 us -> 5.14 us
    pallas_call x19 -> x13, Pallas kernels: 926 us -> 755 us  [call(): pl.pallas_call(kernel, grid=(steps,), out_shape=tuple(shapes) + task_shap...]
    convert_element_type x5 -> x0, other arithmetic: 11.9 us -> none  [wide(): return value.astype(F32)]
where the time goes in v2:
time: 829 us; the launch traced here: 820 us
  Pallas kernels  755 us (91%)
  other arithmetic  58.1 us (7%)
    pallas_call x13, Pallas kernels, call(): pl.pallas_call(kernel, grid=(steps,), out_shape=tuple(shapes) + task_shap...  755 us
    convert_element_type x3, other arithmetic, adamw(): return ((w - 0.02 * step).astype(jnp.bfloat16), m, v)  30.6 us

profile of v2, /device:TPU:0, one launch (start us, length us, event | category | flops | bytes accessed | tf_op | source)
XLA Modules:
  0.0 819.5 jit_solution(3414264224589459093)
XLA Ops:
  0.6 33.0 %norm.1 = (bf16[2048,1280]{1,0:T(8,128)(2,1)}, bf16[1280,2048]{1,0:T(8,128)(2,1)}, bf16[8,160,4864]{2,1,0:T(8,128)(2,1)}) custom-call(bf16[2048,1280]{1,0:T(8,128)(2,1)} %bitcast.45, bf16[2,160,4864]{2,1,0:T(8,128)(2,1)} %refs_4_), custom_call_target="tpu_custom_call" | custom-call | tf_op jit(solution)/shard_map/norm/pallas_call | solution.py:242
  33.6 40.5 %move.1 = (f32[8,128]{1,0:T(8,128)}, bf16[8,160,4864]{2,1,0:T(8,128)(2,1)}, bf16[8,160,4864]{2,1,0:T(8,128)(2,1)}) custom-call(bf16[8,160,4864]{2,1,0:T(8,128)(2,1)} %get-tuple-element.121.refs_0_, bf16[2,160,4864]{2,1,0:T(8,128)(2,1)} %refs_4_.1), custom_call_target="tpu_custom_call", output_to_operand_aliasing={{1}: (0, {})} | custom-call | tf_op jit(solution)/shard_map/move/pallas_call | solution.py:242
  74.1 43.0 %gate.2 = (f32[2048,4864]{1,0:T(8,128)}, bf16[8,160,4864]{2,1,0:T(8,128)(2,1)}, bf16[8,608,1280]{2,1,0:T(8,128)(2,1)}) custom-call(bf16[2048,1280]{1,0:T(8,128)(2,1)} %get-tuple-element.132.refs_0_, bf16[1280,4864]{1,0:T(8,128)(2,1)} %bitcast.40, bf16[8,160,4864]{2,1,0:T(8,128)(2,1)} %get-tuple-element.127.refs_2_, ...), custom_call_target="tpu_custom_call", output_to_operand_aliasing={{1}: (2, {})} | custom-call | flops 25501368320 | tf_op jit(solution)/shard_map/gate/pallas_call | solution.py:242
  117.1 54.1 %up.2 = (f32[2048,4864]{1,0:T(8,128)}, bf16[2048,4864]{1,0:T(8,128)(2,1)}, bf16[4864,2048]{1,0:T(8,128)(2,1)}, bf16[8,608,1280]{2,1,0:T(8,128)(2,1)}, bf16[8,160,4864]{2,1,0:T(8,128)(2,1)}) custom-call(bf16[2048,1280]{1,0:T(8,128)(2,1)} %get-tuple-element.132.refs_0_, bf16[1280,4864]{1,0:T(8,128)(2,1)} %bitcast.49, ...), custom_call_target="tpu_custom_call", output_to_operand_aliasing={{3}: (3, {})} | custom-call | flops 25501368320 | tf_op jit(solution)/shard_map/up/pallas_call | solution.py:242
  171.2 45.8 %down.1 = (bf16[2048,1280]{1,0:T(8,128)(2,1)}, bf16[2048,1280]{1,0:T(8,128)(2,1)}, bf16[1280,2048]{1,0:T(8,128)(2,1)}, bf16[8,160,4864]{2,1,0:T(8,128)(2,1)}, bf16[8,160,4864]{2,1,0:T(8,128)(2,1)}) custom-call(bf16[2048,4864]{1,0:T(8,128)(2,1)} %get-tuple-element.141.refs_0_, bf16[4864,1280]{1,0:T(8,128)(2,1)} %bitcast.55, ...), custom_call_target="tpu_custom_call", output_to_operand_aliasing={{3}: (3, {})} | custom-call | flops 25501368320 | tf_op jit(solution)/shard_map/down/pallas_call | solution.py:242
  217.1 43.2 %gate.3 = (f32[2048,4864]{1,0:T(8,128)}, bf16[8,160,4864]{2,1,0:T(8,128)(2,1)}, bf16[8,608,1280]{2,1,0:T(8,128)(2,1)}) custom-call(bf16[2048,1280]{1,0:T(8,128)(2,1)} %get-tuple-element.157.refs_0_, bf16[1280,4864]{1,0:T(8,128)(2,1)} %bitcast.53, bf16[8,160,4864]{2,1,0:T(8,128)(2,1)} %get-tuple-element.152.refs_2_, ...), custom_call_target="tpu_custom_call", output_to_operand_aliasing={{1}: (2, {})} | custom-call | flops 25501368320 | tf_op jit(solution)/shard_map/gate/pallas_call | solution.py:242
  260.3 54.1 %up.3 = (f32[2048,4864]{1,0:T(8,128)}, bf16[2048,4864]{1,0:T(8,128)(2,1)}, bf16[4864,2048]{1,0:T(8,128)(2,1)}, bf16[8,608,1280]{2,1,0:T(8,128)(2,1)}) custom-call(bf16[2048,1280]{1,0:T(8,128)(2,1)} %get-tuple-element.157.refs_0_, bf16[1280,4864]{1,0:T(8,128)(2,1)} %bitcast.57, ...), custom_call_target="tpu_custom_call", output_to_operand_aliasing={{3}: (3, {})} | custom-call | flops 25501368320 | tf_op jit(solution)/shard_map/up/pallas_call | solution.py:242
  314.4 48.4 %by_down.2 = (bf16[4,608,1280]{2,1,0:T(8,128)(2,1)}, bf16[2,304,1280]{2,1,0:T(8,128)(2,1)}, bf16[2,304,1280]{2,1,0:T(8,128)(2,1)}) custom-call(bf16[4864,2048]{1,0:T(8,128)(2,1)} %get-tuple-element.165.refs_0_, bf16[2048,1280]{1,0:T(8,128)(2,1)} %bitcast.50), custom_call_target="tpu_custom_call" | custom-call | flops 25501368320 | tf_op jit(solution)/shard_map/by_down/pallas_call | solution.py:242
  362.8 0.0 copy-start.7
  362.8 0.0 copy-start.8
  362.8 1.6 slice_bitcast_fusion.2
  364.4 0.2 copy-done.7
  364.7 0.5 copy-done.8
  365.1 2.9 fusion.22
  368.1 112.7 %by_hidden.2 = (bf16[80,4864]{1,0:T(8,128)(2,1)}, bf16[80,4864]{1,0:T(8,128)(2,1)}, f32[160,4864]{1,0:T(8,128)}, bf16[80,4864]{1,0:T(8,128)(2,1)}, bf16[80,4864]...) custom-call(bf16[2048,1280]{1,0:T(8,128)(2,1)} %bitcast.51, ...), custom_call_target="tpu_custom_call" | custom-call | flops 76504104960 | tf_op jit(solution)/shard_map/by_hidden/pallas_call | solution.py:242
  480.8 3.6 fusion.16.refs_6_
  484.4 41.0 %by_a.2 = (bf16[2048,1280]{1,0:T(8,128)(2,1)}, bf16[80,4864]{1,0:T(8,128)(2,1)}, bf16[80,4864]{1,0:T(8,128)(2,1)}, bf16[80,4864]{1,0:T(8,128)(2,1)}, bf16[80,486...) custom-call(bf16[2048,4864]{1,0:T(8,128)(2,1)} %get-tuple-element.185.refs_0_, bf16[1280,4864]{1,0:T(8,128)(2,1)} %bitcast.54, ...), custom_call_target="tpu_custom_call" | custom-call | flops 25501368320 | tf_op jit(solution)/shard_map/by_a/pallas_call | solution.py:242
  525.5 2.4 fusion.20
  527.9 0.4 copy-done.6
  528.3 0.2 copy-done.13
  528.5 0.2 copy-done.14
  528.7 1.4 add_convert_fusion.4.refs_2_
  530.1 1.0 copy-done.5
  531.2 0.2 copy-done.11
  531.3 0.2 copy-done.12
  531.6 1.4 add_convert_fusion.5.refs_5_
  533.0 41.0 %by_a.3 = (bf16[2048,1280]{1,0:T(8,128)(2,1)}, bf16[160,4864]{1,0:T(8,128)(2,1)}) custom-call(bf16[2048,4864]{1,0:T(8,128)(2,1)} %get-tuple-element.196.refs_0_, bf16[1280,4864]{1,0:T(8,128)(2,1)} %bitcast.58, bf16[2048,1280]{1,0:T(8,128)(2,1)} %get-tuple-element.198.refs_2_, bf16[2048,1280]{1,0:T(8,128)(2,1)} %get-tuple-element.199.refs_3_, ...), custom_call_target="tpu_custom_call" | custom-call | flops 25501368320 | tf_op jit(solution)/shard_map/by_a/pallas_call | solution.py:242
  574.0 3.4 fusion.17
  577.4 48.5 %by_down.3 = (bf16[4,608,1280]{2,1,0:T(8,128)(2,1)}, bf16[2,304,1280]{2,1,0:T(8,128)(2,1)}, bf16[2,304,1280]{2,1,0:T(8,128)(2,1)}, bf16[160,4864]{1,0:T(8,128)(2,1)}) custom-call(bf16[4864,2048]{1,0:T(8,128)(2,1)} %get-tuple-element.208.refs_0_, bf16[2048,1280]{1,0:T(8,128)(2,1)} %get-tuple-element.214.refs_1_.refs_0_, ...), custom_call_target="tpu_custom_call" | custom-call | flops 25501368320 | tf_op jit(solution)/shard_map/by_down/pallas_call | solution.py:242
  625.9 3.5 fusion.18
  629.4 0.1 slice_bitcast_fusion.1
  629.5 0.0 copy-done.9
  629.5 3.0 fusion.24
  632.4 0.1 slice_bitcast_fusion
  632.5 3.5 convert_add_fusion.refs_7_
  636.0 149.5 %by_hidden.3 = (bf16[160,4864]{1,0:T(8,128)(2,1)}, bf16[160,4864]{1,0:T(8,128)(2,1)}, bf16[608,1280]{1,0:T(8,128)(2,1)}, bf16[608,1280]{1,0:T(8,128)(2,1)}) custom-call(bf16[2048,1280]{1,0:T(8,128)(2,1)} %get-tuple-element.214.refs_1_.refs_0_, bf16[4864,1280]{1,0:T(8,128)(2,1)} %bitcast.56, f32[2048,4864]{1,0:T(8,128)} %get-tuple-element.216.refs_2_, ...), custom_call_target="tpu_custom_call" | custom-call | flops 76504104960 | tf_op jit(solution)/shard_map/by_hidden/pallas_call | solution.py:242
  785.5 0.0 copy-start.4
  785.5 0.0 slice-start
  785.5 2.4 fusion.19
  787.9 0.4 copy-done.4
  788.3 10.7 %fusion.10 = (bf16[2,608,1280]{2,1,0:T(8,128)(2,1)}, f32[2,608,1280]{2,1,0:T(8,128)}, f32[2,608,1280]{2,1,0:T(8,128)}) fusion(bf16[2,608,1280]{2,1,0:T(8,128)(2,1)S(1)} %copy-done.4, bf16[1,608,1280]{2,1,0:T(8,128)(2,1)S(1)} %fusion.20, bf16[1,608,1280]{2,1,0:T(8,128)(2,1)S(1)} %fusion.19, f32[2,608,1280]{2,1,0:T(8,128)} %param.21, f32[2,608,1280]{2,1,0:T(8,128)} %param.18), kind=kLoop, calls=%fused_computation.22 | loop fusion | flops 29573120 | bytes 34242560 | tf_op jit(solution)/shard_map/convert_element_type | solution.py:31
  799.1 0.0 copy-start
  799.1 0.0 copy-start.2
  799.1 0.0 slice-start.3
  799.1 10.5 %fusion.6 = (bf16[2,160,4864]{2,1,0:T(8,128)(2,1)}, f32[2,160,4864]{2,1,0:T(8,128)}, f32[2,160,4864]{2,1,0:T(8,128)}) fusion(bf16[2,160,4864]{2,1,0:T(8,128)(2,1)S(1)} %copy-done.1, bf16[1,160,4864]{2,1,0:T(8,128)(2,1)S(1)} %copy-done.3, bf16[1,160,4864]{2,1,0:T(8,128)(2,1)} %bitcast.48, f32[2,160,4864]{2,1,0:T(8,128)S(1)} %bitcast.42, f32[2,160,4864]{2,1,0:T(8,128)} %param.17), kind=kLoop, calls=%fused_computation.18 | loop fusion | flops 29573120 | bytes 34242560 | tf_op jit(solution)/shard_map/convert_element_type | solution.py:31
  809.7 0.0 copy-done.2
  809.7 0.0 slice-done.3
  809.7 9.4 %fusion.2 = (bf16[2,160,4864]{2,1,0:T(8,128)(2,1)}, f32[2,160,4864]{2,1,0:T(8,128)}, f32[2,160,4864]{2,1,0:T(8,128)}) fusion(bf16[2,160,4864]{2,1,0:T(8,128)(2,1)S(1)} %copy-done, bf16[1,160,4864]{2,1,0:T(8,128)(2,1)S(1)} %copy-done.2, bf16[1,160,4864]{2,1,0:T(8,128)(2,1)} %bitcast.47, f32[2,160,4864]{2,1,0:T(8,128)S(1)} %bitcast.44, f32[2,160,4864]{2,1,0:T(8,128)} %param.16), kind=kLoop, calls=%fused_computation.14 | loop fusion | flops 29573120 | bytes 34242560 | tf_op jit(solution)/shard_map/convert_element_type | solution.py:31
  (21 shorter events, 0.0 us)
Async XLA Ops:
  362.8 1.9 copy-start.7
  362.8 2.3 copy-start.8
  525.5 2.8 copy-start.6
  525.5 3.0 copy-start.13
  525.5 3.2 copy-start.14
  528.7 2.4 copy-start.5
  528.7 2.6 copy-start.11
  528.7 2.9 copy-start.12
  625.9 3.5 copy-start.10
  625.9 3.6 copy-start.9
  785.5 2.8 copy-start.4
  785.5 13.6 %slice-start = ((s8[6225920]{0:T(1024)(128)(4,1)}), s8[4194304]{0:T(1024)(128)(4,1)S(1)}, s32[]{:S(2)}) async-start(s8[6225920]{0:T(1024)(128)(4,1)} %bitcast.41), calls=%async_computation | async-start | bytes 8388608
  788.3 10.8 %copy-start.1 = (bf16[2,160,4864]{2,1,0:T(8,128)(2,1)S(1)}, bf16[2,160,4864]{2,1,0:T(8,128)(2,1)}, u32[]{:S(2)}) copy-start(bf16[2,160,4864]{2,1,0:T(8,128)(2,1)} %refs_4_.1) | copy-start | bytes 9338884
  788.3 10.8 %copy-start.3 = (bf16[1,160,4864]{2,1,0:T(8,128)(2,1)S(1)}, bf16[1,160,4864]{2,1,0:T(8,128)(2,1)}, u32[]{:S(2)}) copy-start(bf16[1,160,4864]{2,1,0:T(8,128)(2,1)} %fusion.18) | copy-start | bytes 4669444
  788.3 10.8 %slice-start.1 = ((s8[6225920]{0:T(1024)(128)(4,1)}), s8[2031616]{0:T(1024)(128)(4,1)S(1)}, s32[]{:S(2)}) async-start(s8[6225920]{0:T(1024)(128)(4,1)} %bitcast.41), calls=%async_computation.1 | async-start | bytes 4063232
  799.0 10.6 %slice-start.2 = ((s8[6225920]{0:T(1024)(128)(4,1)}), s8[4194304]{0:T(1024)(128)(4,1)S(1)}, s32[]{:S(2)}) async-start(s8[6225920]{0:T(1024)(128)(4,1)} %bitcast.43), calls=%async_computation.2 | async-start | bytes 8388608
  799.1 10.6 %copy-start = (bf16[2,160,4864]{2,1,0:T(8,128)(2,1)S(1)}, bf16[2,160,4864]{2,1,0:T(8,128)(2,1)}, u32[]{:S(2)}) copy-start(bf16[2,160,4864]{2,1,0:T(8,128)(2,1)} %refs_4_) | copy-start | bytes 9338884
  799.1 10.6 %copy-start.2 = (bf16[1,160,4864]{2,1,0:T(8,128)(2,1)S(1)}, bf16[1,160,4864]{2,1,0:T(8,128)(2,1)}, u32[]{:S(2)}) copy-start(bf16[1,160,4864]{2,1,0:T(8,128)(2,1)} %fusion.17) | copy-start | bytes 4669444
  799.1 10.6 %slice-start.3 = ((s8[6225920]{0:T(1024)(128)(4,1)}), s8[2031616]{0:T(1024)(128)(4,1)S(1)}, s32[]{:S(2)}) async-start(s8[6225920]{0:T(1024)(128)(4,1)} %bitcast.43), calls=%async_computation.3 | async-start | bytes 4063232

commit v3 on v2

--- a/solution.py
+++ b/solution.py
@@ -90,7 +90,7 @@
 
 
 class Gather2:
-    ways, copies, when, alias = ("x", "y", "z", "c"), 11, (0.5,), {0: 0}
+    ways, copies, when, alias = ("x", "y", "z", "c"), 11, (0.45,), {0: 0}
     held, scratch = False, ()
 
     def __init__(self, so_far):
@@ -145,7 +145,7 @@
 
 
 class LastHops:
-    ways, alias, held, start, piece = ("x", "y", "z"), {}, False, 8, 64
+    ways, alias, held, start, piece = ("x", "y", "z"), {}, False, 5, 32
 
     def __init__(self, to_y, to_x, part):
         self.pieces = [(at, min(self.piece, part.shape[0] - at)) for at in range(0, part.shape[0], self.piece)]
@@ -188,13 +188,25 @@
     def call(self, name, body, steps, operands, in_specs, shapes, out_specs, scratch=(), ways=(), tasks=(), flops=0):
         tasks = list(tasks)
         ways = tuple(sorted(set(ways).union(*(t.ways for t in tasks))))
+        resident = [n for n, spec in enumerate(in_specs) if isinstance(spec, Resident)]
         counts = [len(operands), sum(len(t.operands) for t in tasks), len(shapes), sum(len(t.shapes) for t in tasks), len(scratch)]
 
         def kernel(*refs):
             refs = list(refs)
             ins, task_ins, outs, task_outs, own = ([refs.pop(0) for _ in range(n)] for n in counts)
             i = pl.program_id(0)
-            held = []
+            held, loads = [], []
+            for n in resident:
+                into, sem = refs.pop(0), refs.pop(0)
+                loads.append(pltpu.make_async_copy(ins[n], into, sem))
+                ins[n] = into
+
+            if loads:
+                @pl.when(i == 0)
+                def _():
+                    for each in loads:
+                        each.start()
+
             for t in tasks:
                 a, task_ins = task_ins[: len(t.operands)], task_ins[len(t.operands) :]
                 b, task_outs = task_outs[: len(t.shapes)], task_outs[len(t.shapes) :]
@@ -211,6 +223,12 @@
                     for t, sends, a, b, local in held:
                         t.stage(0, sends, a, b, local)
 
+            if loads:
+                @pl.when(i == 0)
+                def _():
+                    for each in loads:
+                        each.wait()
+
             for t, sends, a, b, local in held:
                 for number, when in enumerate(t.when):
                     @pl.when(i == (when if isinstance(when, int) else int(steps * when)))
@@ -227,6 +245,8 @@
                         t.stage(len(t.when) + 1, sends, a, b, local)
 
         sems = []
+        for n in resident:
+            sems += [pltpu.VMEM(in_specs[n].dims, operands[n].dtype), pltpu.SemaphoreType.DMA]
         for t in tasks:
             sems += [pltpu.SemaphoreType.DMA((t.copies,)), pltpu.SemaphoreType.DMA((t.copies,)), pltpu.SemaphoreType.DMA, *t.scratch]
         task_operands = tuple(o for t in tasks for o in t.operands)
@@ -243,7 +263,7 @@
             kernel,
             grid=(steps,),
             out_shape=tuple(shapes) + task_shapes,
-            in_specs=list(in_specs) + [t.spec if t.held else ANY for t in tasks for o in t.operands],
+            in_specs=[ANY if isinstance(spec, Resident) else spec for spec in in_specs] + [t.spec if t.held else ANY for t in tasks for o in t.operands],
             out_specs=list(out_specs) + [ANY] * len(task_shapes),
             scratch_shapes=list(scratch) + sems,
             name=name,
@@ -262,8 +282,9 @@
     return jax.ShapeDtypeStruct(dims, dtype)
 
 
-def held_block(dims):
-    return pl.BlockSpec(dims, lambda i: (0,) * len(dims), pipeline_mode=pl.Buffered(1))
+class Resident:
+    def __init__(self, dims):
+        self.dims = dims
 
 
 def dot(a, b, contract=(1, 0)):
@@ -296,7 +317,7 @@
         outs[0][...] = dot(ins[0][...], ins[1][...])
 
     return line.call(
-        "gate", body, f // WIDTH, (a, w), [held_block((t, d)), pl.BlockSpec((d, WIDTH), lambda i: (0, i))],
+        "gate", body, f // WIDTH, (a, w), [Resident((t, d)), pl.BlockSpec((d, WIDTH), lambda i: (0, i))],
         (shape(t, f, dtype=F32),), [pl.BlockSpec((t, WIDTH), lambda i: (0, i))], tasks=tasks, flops=2 * t * d * f,
     )
 
@@ -316,7 +337,8 @@
             outs[2][s] = act.T
 
     return line.call(
-        "up", body, t // TALL, (a, w, gate), [rows(d), held_block((d, f)), rows(f)],
+        "up", body, t // TALL, (a, w, gate),
+        [rows(d), pl.BlockSpec((d, f), lambda i: (0, 0), pipeline_mode=pl.Buffered(1)), rows(f)],
         (shape(t, f, dtype=F32), shape(t, f), shape(f, t)), [rows(f), rows(f), pl.BlockSpec((f, TALL), lambda i: (0, i))],
         tasks=tasks, flops=2 * t * d * f,
     )
@@ -335,7 +357,7 @@
         outs[2][...] = a.T
 
     return line.call(
-        "down", body, t // TALL, (act, w, h), [rows(f), held_block((f, d)), rows(d)], (shape(t, d), shape(t, d), shape(d, t)),
+        "down", body, t // TALL, (act, w, h), [rows(f), Resident((f, d)), rows(d)], (shape(t, d), shape(t, d), shape(d, t)),
         [rows(d), rows(d), pl.BlockSpec((d, TALL), lambda i: (0, i))], tasks=tasks, flops=2 * t * d * f,
     )
 
@@ -353,7 +375,7 @@
         outs[0][...] = new
 
     return line.call(
-        "by_a", body, t // TALL, (by, w) + more, [rows(f), held_block((d, f))] + [rows(d)] * len(more), (shape(t, d),), [rows(d)],
+        "by_a", body, t // TALL, (by, w) + more, [rows(f), Resident((d, f))] + [rows(d)] * len(more), (shape(t, d),), [rows(d)],
         tasks=tasks, flops=2 * t * d * f,
     )
 
@@ -465,7 +487,7 @@
         out_specs = [at(half, WIDTH), at(half, WIDTH), at(rows, WIDTH)] * 2 + [tile, tile]
     return line.call(
         "by_hidden", body, tiles + 2 * hops, (by_h, w, gate, up, a_t),
-        [held_block((t, d)), pl.BlockSpec((WIDTH, d), lambda i: (jnp.minimum(i, last), 0)), tile, tile, held_block((d, t))],
+        [Resident((t, d)), pl.BlockSpec((WIDTH, d), lambda i: (jnp.minimum(i, last), 0)), tile, tile, Resident((d, t))],
         shapes, out_specs,
         scratch=[
             pltpu.VMEM((t, both), BF16),
@@ -493,8 +515,7 @@
         return (there_x * 2 + there_y) * 2 + jnp.where(i % 2 == 0, 1 - c, c), 0
 
     def body(i, ins, outs, own):
-        mine, theirs, pair, send_sem, recv_sem, hop_send, hop_recv = own
-        rx, ry = outs[1:]
+        mine, theirs, pair, rx, ry, send_sem, recv_sem, hop_send, hop_recv = own
 
         def remote(way, src, dst, send, recv):
             return pltpu.make_async_remote_copy(
@@ -528,19 +549,22 @@
             sent(n).wait()
             total = narrow(new + wide(theirs[n]))
             pair[n] = total
-            outs[0][0] = total
 
         @pl.when(i == 7)
         def _():
             for each in hop:
                 each.wait()
-
-    hopped = shape(2, half, d)
+            outs[0][...] = narrow(wide(pair[2, low]) + wide(rx[1]))
+            outs[1][...] = narrow(wide(pair[1, high]) + wide(ry[1]))
+            outs[2][low] = wide(pair[3, low]) + wide(rx[0])
+            outs[2][high] = wide(pair[3, high]) + wide(ry[0])
+
+    whole = lambda n: pl.BlockSpec((n, d), lambda i: (0, 0))
     return line.call(
-        "by_down", body, 8, (act_t, by_h), [pl.BlockSpec((rows, t), block), held_block((t, d))],
-        (shape(4, rows, d), hopped, hopped), [pl.BlockSpec((1, rows, d), lambda i: (i // 2, 0, 0)), ANY, ANY],
+        "by_down", body, 8, (act_t, by_h), [pl.BlockSpec((rows, t), block), Resident((t, d))],
+        (shape(half, d), shape(half, d), shape(rows, d, dtype=F32)), [whole(half), whole(half), whole(rows)],
         scratch=[
-            *[pltpu.VMEM((4, rows, d), BF16)] * 3,
+            *[pltpu.VMEM((4, rows, d), BF16)] * 3, *[pltpu.VMEM((2, half, d), BF16)] * 2,
             *[pltpu.SemaphoreType.DMA((4,))] * 4,
         ],
         ways=("c", "x", "y"), tasks=tasks, flops=2 * t * d * f,
@@ -552,12 +576,6 @@
         outs[0][...] = jnp.zeros_like(outs[0])
 
     return line.call("move", body, 1, (), [], (shape(8, 128, dtype=F32),), [pl.BlockSpec((8, 128), lambda i: (0, 0))], tasks=tasks)[1]
-
-
-def second(sums, rx, ry):
-    half = sums.shape[1] // 2
-    to_y, to_x = wide(sums[2, :half]) + wide(rx[1]), wide(sums[1, half:]) + wide(ry[1])
-    return narrow(to_y), narrow(to_x), wide(sums[3]) + wide(jnp.concatenate([rx[0], ry[0]]))
 
 
 def solution(mesh):
@@ -581,8 +599,7 @@
         (up1, act1, act1t), [[wd1]] = up_call(line, a1, wu1, gate1, [Gather2(d)])
         wd1 = flat(wd1)
 
-        down1, _ = by_down_call(line, act1t, dy, [])
-        to_y, to_x, part = second(*down1)
+        (to_y, to_x, part), _ = by_down_call(line, act1t, dy, [])
         (gy, gx, gpart, uy, ux, upart, dg1, du1), [(from_y, from_x)] = by_hidden_call(
             line, dy, wd1, gate1, up1, a1t, [Hops(("y", to_y), ("x", to_x))], False
         )
@@ -594,7 +611,7 @@
         bg1, bu1 = joined(gpart, gfy, gfx), joined(upart, ufy, ufx)
         (by_h,), [(zg1,)] = by_a_call(line, du1, wu1, (da, h1, dy), [Hops(("z", bg1))])
         down0, [(zu1,)] = by_down_call(line, act0t, by_h, [Hops(("z", bu1))])
-        (g0, u0), [(bd0, zd0)] = by_hidden_call(line, by_h, wd0, gate0, up0, a0t, [LastHops(*second(*down0))], True)
+        (g0, u0), [(bd0, zd0)] = by_hidden_call(line, by_h, wd0, gate0, up0, a0t, [LastHops(*down0)], True)
 
         total = lambda b, z: narrow(wide(b) + wide(z))
         gradients = [

time: 829 us -> 809 us (0.976)
  Pallas kernels: 755 us -> 745 us
    pallas_call x13, Pallas kernels: 755 us -> 745 us  [call(): pl.pallas_call(kernel, grid=(steps,), out_shape=tuple(shapes) + task_shap...]
where the time goes in v3:
time: 809 us; the launch traced here: 799 us
  Pallas kernels  745 us (92%)
  other arithmetic  52.3 us (6%)
    pallas_call x13, Pallas kernels, call(): pl.pallas_call(kernel, grid=(steps,), out_shape=tuple(shapes) + task_shap...  745 us
    convert_element_type x3, other arithmetic, adamw(): return ((w - 0.02 * step).astype(jnp.bfloat16), m, v)  32.1 us

profile of v3, /device:TPU:0, one launch (start us, length us, event | category | flops | bytes accessed | tf_op | source)
XLA Modules:
  0.0 799.3 jit_solution(10929464326849714716)
XLA Ops:
  0.6 33.0 %norm.1 = (bf16[2048,1280]{1,0:T(8,128)(2,1)}, bf16[1280,2048]{1,0:T(8,128)(2,1)}, bf16[8,160,4864]{2,1,0:T(8,128)(2,1)}) custom-call(bf16[2048,1280]{1,0:T(8,128)(2,1)} %bitcast.21, bf16[2,160,4864]{2,1,0:T(8,128)(2,1)} %refs_4_), custom_call_target="tpu_custom_call" | custom-call | tf_op jit(solution)/shard_map/norm/pallas_call | solution.py:262
  33.6 40.5 %move.1 = (f32[8,128]{1,0:T(8,128)}, bf16[8,160,4864]{2,1,0:T(8,128)(2,1)}, bf16[8,160,4864]{2,1,0:T(8,128)(2,1)}) custom-call(bf16[8,160,4864]{2,1,0:T(8,128)(2,1)} %get-tuple-element.121.refs_0_, bf16[2,160,4864]{2,1,0:T(8,128)(2,1)} %refs_4_.1), custom_call_target="tpu_custom_call", output_to_operand_aliasing={{1}: (0, {})} | custom-call | tf_op jit(solution)/shard_map/move/pallas_call | solution.py:262
  74.1 41.6 %gate.2 = (f32[2048,4864]{1,0:T(8,128)}, bf16[8,160,4864]{2,1,0:T(8,128)(2,1)}, bf16[8,608,1280]{2,1,0:T(8,128)(2,1)}) custom-call(bf16[2048,1280]{1,0:T(8,128)(2,1)} %get-tuple-element.132.refs_0_, bf16[1280,4864]{1,0:T(8,128)(2,1)} %bitcast.18, bf16[8,160,4864]{2,1,0:T(8,128)(2,1)} %get-tuple-element.127.refs_2_, ...), custom_call_target="tpu_custom_call", output_to_operand_aliasing={{1}: (2, {})} | custom-call | flops 25501368320 | tf_op jit(solution)/shard_map/gate/pallas_call | solution.py:262
  115.7 54.1 %up.2 = (f32[2048,4864]{1,0:T(8,128)}, bf16[2048,4864]{1,0:T(8,128)(2,1)}, bf16[4864,2048]{1,0:T(8,128)(2,1)}, bf16[8,608,1280]{2,1,0:T(8,128)(2,1)}, bf16[8,160,4864]{2,1,0:T(8,128)(2,1)}) custom-call(bf16[2048,1280]{1,0:T(8,128)(2,1)} %get-tuple-element.132.refs_0_, bf16[1280,4864]{1,0:T(8,128)(2,1)} %bitcast.25, ...), custom_call_target="tpu_custom_call", output_to_operand_aliasing={{3}: (3, {})} | custom-call | flops 25501368320 | tf_op jit(solution)/shard_map/up/pallas_call | solution.py:262
  169.8 42.6 %down.1 = (bf16[2048,1280]{1,0:T(8,128)(2,1)}, bf16[2048,1280]{1,0:T(8,128)(2,1)}, bf16[1280,2048]{1,0:T(8,128)(2,1)}, bf16[8,160,4864]{2,1,0:T(8,128)(2,1)}, bf16[8,160,4864]{2,1,0:T(8,128)(2,1)}) custom-call(bf16[2048,4864]{1,0:T(8,128)(2,1)} %get-tuple-element.141.refs_0_, bf16[4864,1280]{1,0:T(8,128)(2,1)} %bitcast.31, ...), custom_call_target="tpu_custom_call", output_to_operand_aliasing={{3}: (3, {})} | custom-call | flops 25501368320 | tf_op jit(solution)/shard_map/down/pallas_call | solution.py:262
  212.4 41.4 %gate.3 = (f32[2048,4864]{1,0:T(8,128)}, bf16[8,160,4864]{2,1,0:T(8,128)(2,1)}, bf16[8,608,1280]{2,1,0:T(8,128)(2,1)}) custom-call(bf16[2048,1280]{1,0:T(8,128)(2,1)} %get-tuple-element.157.refs_0_, bf16[1280,4864]{1,0:T(8,128)(2,1)} %bitcast.29, bf16[8,160,4864]{2,1,0:T(8,128)(2,1)} %get-tuple-element.152.refs_2_, ...), custom_call_target="tpu_custom_call", output_to_operand_aliasing={{1}: (2, {})} | custom-call | flops 25501368320 | tf_op jit(solution)/shard_map/gate/pallas_call | solution.py:262
  253.8 54.2 %up.3 = (f32[2048,4864]{1,0:T(8,128)}, bf16[2048,4864]{1,0:T(8,128)(2,1)}, bf16[4864,2048]{1,0:T(8,128)(2,1)}, bf16[8,608,1280]{2,1,0:T(8,128)(2,1)}) custom-call(bf16[2048,1280]{1,0:T(8,128)(2,1)} %get-tuple-element.157.refs_0_, bf16[1280,4864]{1,0:T(8,128)(2,1)} %bitcast.33, ...), custom_call_target="tpu_custom_call", output_to_operand_aliasing={{3}: (3, {})} | custom-call | flops 25501368320 | tf_op jit(solution)/shard_map/up/pallas_call | solution.py:262
  307.9 50.3 %by_down.2 = (bf16[304,1280]{1,0:T(8,128)(2,1)}, bf16[304,1280]{1,0:T(8,128)(2,1)}, f32[608,1280]{1,0:T(8,128)}) custom-call(bf16[4864,2048]{1,0:T(8,128)(2,1)} %get-tuple-element.165.refs_0_, bf16[2048,1280]{1,0:T(8,128)(2,1)} %bitcast.26), custom_call_target="tpu_custom_call" | custom-call | flops 25501368320 | tf_op jit(solution)/shard_map/by_down/pallas_call | solution.py:262
  358.3 113.1 %by_hidden.2 = (bf16[80,4864]{1,0:T(8,128)(2,1)}, bf16[80,4864]{1,0:T(8,128)(2,1)}, f32[160,4864]{1,0:T(8,128)}, bf16[80,4864]{1,0:T(8,128)(2,1)}, bf16[80,4864]...) custom-call(bf16[2048,1280]{1,0:T(8,128)(2,1)} %bitcast.27, ...), custom_call_target="tpu_custom_call" | custom-call | flops 76504104960 | tf_op jit(solution)/shard_map/by_hidden/pallas_call | solution.py:262
  471.4 3.8 add_convert_fusion.6.refs_6_
  475.1 37.8 %by_a.2 = (bf16[2048,1280]{1,0:T(8,128)(2,1)}, bf16[80,4864]{1,0:T(8,128)(2,1)}, bf16[80,4864]{1,0:T(8,128)(2,1)}, bf16[80,4864]{1,0:T(8,128)(2,1)}, bf16[80,486...) custom-call(bf16[2048,4864]{1,0:T(8,128)(2,1)} %get-tuple-element.185.refs_0_, bf16[1280,4864]{1,0:T(8,128)(2,1)} %bitcast.30, ...), custom_call_target="tpu_custom_call" | custom-call | flops 25501368320 | tf_op jit(solution)/shard_map/by_a/pallas_call | solution.py:262
  512.9 0.0 copy-start.5
  512.9 2.4 fusion.18
  515.3 0.4 copy-done.5
  515.7 5.0 add_convert_fusion.4
  520.7 37.9 %by_a.3 = (bf16[2048,1280]{1,0:T(8,128)(2,1)}, bf16[160,4864]{1,0:T(8,128)(2,1)}) custom-call(bf16[2048,4864]{1,0:T(8,128)(2,1)} %get-tuple-element.196.refs_0_, bf16[1280,4864]{1,0:T(8,128)(2,1)} %bitcast.34, bf16[2048,1280]{1,0:T(8,128)(2,1)} %get-tuple-element.198.refs_2_, bf16[2048,1280]{1,0:T(8,128)(2,1)} %get-tuple-element.199.refs_3_, ...), custom_call_target="tpu_custom_call" | custom-call | flops 25501368320 | tf_op jit(solution)/shard_map/by_a/pallas_call | solution.py:262
  558.6 3.4 fusion.15
  562.0 50.2 %by_down.3 = (bf16[304,1280]{1,0:T(8,128)(2,1)}, bf16[304,1280]{1,0:T(8,128)(2,1)}, f32[608,1280]{1,0:T(8,128)}, bf16[160,4864]{1,0:T(8,128)(2,1)}) custom-call(bf16[4864,2048]{1,0:T(8,128)(2,1)} %get-tuple-element.208.refs_0_, bf16[2048,1280]{1,0:T(8,128)(2,1)} %get-tuple-element.214.refs_1_.refs_0_, bf16[160,4864]{1,0:T(8,128)(2,1)} %get-tuple-element.210.refs_2_), custom_call_target="tpu_custom_call" | custom-call | flops 25501368320 | tf_op jit(solution)/shard_map/by_down/pallas_call | solution.py:262
  612.2 3.4 fusion.16
  615.5 148.3 %by_hidden.3 = (bf16[160,4864]{1,0:T(8,128)(2,1)}, bf16[160,4864]{1,0:T(8,128)(2,1)}, bf16[608,1280]{1,0:T(8,128)(2,1)}, bf16[608,1280]{1,0:T(8,128)(2,1)}) custom-call(bf16[2048,1280]{1,0:T(8,128)(2,1)} %get-tuple-element.214.refs_1_.refs_0_, bf16[4864,1280]{1,0:T(8,128)(2,1)} %bitcast.32, f32[2048,4864]{1,0:T(8,128)} %get-tuple-element.216.refs_2_, ...), custom_call_target="tpu_custom_call" | custom-call | flops 76504104960 | tf_op jit(solution)/shard_map/by_hidden/pallas_call | solution.py:262
  763.8 0.0 copy-start.4
  763.8 2.4 fusion.17
  766.2 0.4 copy-done.4
  766.6 0.0 copy-start.1
  766.6 0.0 copy-start.3
  766.6 0.0 copy-start.7
  766.6 0.0 slice-start
  766.6 11.9 %fusion.10 = (bf16[2,608,1280]{2,1,0:T(8,128)(2,1)}, f32[2,608,1280]{2,1,0:T(8,128)}, f32[2,608,1280]{2,1,0:T(8,128)}) fusion(bf16[2,608,1280]{2,1,0:T(8,128)(2,1)S(1)} %copy-done.4, bf16[1,608,1280]{2,1,0:T(8,128)(2,1)S(1)} %fusion.18, bf16[1,608,1280]{2,1,0:T(8,128)(2,1)S(1)} %fusion.17, f32[2,608,1280]{2,1,0:T(8,128)} %param.21, f32[2,608,1280]{2,1,0:T(8,128)} %param.18), kind=kLoop, calls=%fused_computation.22 | loop fusion | flops 29573120 | bytes 34242560 | tf_op jit(solution)/shard_map/convert_element_type | solution.py:31
  778.5 0.0 copy-done.1
  778.5 0.0 copy-done.3
  778.5 0.0 copy-done.7
  778.5 0.0 copy-start
  778.5 0.0 copy-start.2
  778.6 0.0 slice-start.1
  778.6 0.0 copy-start.6
  778.6 11.1 %fusion.6 = (bf16[2,160,4864]{2,1,0:T(8,128)(2,1)}, f32[2,160,4864]{2,1,0:T(8,128)}, f32[2,160,4864]{2,1,0:T(8,128)}) fusion(bf16[2,160,4864]{2,1,0:T(8,128)(2,1)S(1)} %copy-done.1, bf16[1,160,4864]{2,1,0:T(8,128)(2,1)S(1)} %copy-done.3, bf16[1,160,4864]{2,1,0:T(8,128)(2,1)S(1)} %bitcast.24, f32[2,160,4864]{2,1,0:T(8,128)} %param.20, f32[2,160,4864]{2,1,0:T(8,128)} %param.17), kind=kLoop, calls=%fused_computation.18 | loop fusion | flops 29573120 | bytes 34242560 | tf_op jit(solution)/shard_map/convert_element_type | solution.py:31
  789.7 0.0 slice-done
  789.7 0.0 copy-done
  789.7 0.0 copy-done.2
  789.7 0.0 slice-done.1
  789.7 0.0 copy-done.6
  789.8 9.1 %fusion.2 = (bf16[2,160,4864]{2,1,0:T(8,128)(2,1)}, f32[2,160,4864]{2,1,0:T(8,128)}, f32[2,160,4864]{2,1,0:T(8,128)}) fusion(bf16[2,160,4864]{2,1,0:T(8,128)(2,1)S(1)} %copy-done, bf16[1,160,4864]{2,1,0:T(8,128)(2,1)S(1)} %copy-done.2, bf16[1,160,4864]{2,1,0:T(8,128)(2,1)S(1)} %bitcast.23, f32[2,160,4864]{2,1,0:T(8,128)S(1)} %bitcast.20, ...), kind=kLoop, calls=%fused_computation.14 | loop fusion | flops 29573120 | bytes 34242560 | tf_op jit(solution)/shard_map/convert_element_type | solution.py:31
  (1 shorter events, 0.0 us)
Async XLA Ops:
  512.9 2.8 copy-start.5
  763.8 2.8 copy-start.4
  766.6 11.9 %copy-start.1 = (bf16[2,160,4864]{2,1,0:T(8,128)(2,1)S(1)}, bf16[2,160,4864]{2,1,0:T(8,128)(2,1)}, u32[]{:S(2)}) copy-start(bf16[2,160,4864]{2,1,0:T(8,128)(2,1)} %refs_4_.1) | copy-start | bytes 9338884
  766.6 11.9 %copy-start.3 = (bf16[1,160,4864]{2,1,0:T(8,128)(2,1)S(1)}, bf16[1,160,4864]{2,1,0:T(8,128)(2,1)}, u32[]{:S(2)}) copy-start(bf16[1,160,4864]{2,1,0:T(8,128)(2,1)} %fusion.16) | copy-start | bytes 4669444
  766.6 11.9 %copy-start.7 = (bf16[160,4864]{1,0:T(8,128)(2,1)S(1)}, bf16[160,4864]{1,0:T(8,128)(2,1)}, u32[]{:S(2)}) copy-start(bf16[160,4864]{1,0:T(8,128)(2,1)} %get-tuple-element.224) | copy-start | bytes 4669444
  766.6 23.1 %slice-start = ((s8[6225920]{0:T(1024)(128)(4,1)}), s8[4194304]{0:T(1024)(128)(4,1)S(1)}, s32[]{:S(2)}) async-start(s8[6225920]{0:T(1024)(128)(4,1)} %bitcast.19), calls=%async_computation | async-start | bytes 8388608
  778.5 11.2 %copy-start = (bf16[2,160,4864]{2,1,0:T(8,128)(2,1)S(1)}, bf16[2,160,4864]{2,1,0:T(8,128)(2,1)}, u32[]{:S(2)}) copy-start(bf16[2,160,4864]{2,1,0:T(8,128)(2,1)} %refs_4_) | copy-start | bytes 9338884
  778.5 11.2 %copy-start.2 = (bf16[1,160,4864]{2,1,0:T(8,128)(2,1)S(1)}, bf16[1,160,4864]{2,1,0:T(8,128)(2,1)}, u32[]{:S(2)}) copy-start(bf16[1,160,4864]{2,1,0:T(8,128)(2,1)} %fusion.15) | copy-start | bytes 4669444
  778.6 11.2 %slice-start.1 = ((s8[6225920]{0:T(1024)(128)(4,1)}), s8[2031616]{0:T(1024)(128)(4,1)S(1)}, s32[]{:S(2)}) async-start(s8[6225920]{0:T(1024)(128)(4,1)} %bitcast.19), calls=%async_computation.1 | async-start | bytes 4063232
  778.6 11.2 %copy-start.6 = (bf16[160,4864]{1,0:T(8,128)(2,1)S(1)}, bf16[160,4864]{1,0:T(8,128)(2,1)}, u32[]{:S(2)}) copy-start(bf16[160,4864]{1,0:T(8,128)(2,1)} %get-tuple-element.222) | copy-start | bytes 4669444
